TPU v7x, 32 devices: a whole 2x2x4 slice. The times are simulated.
32 devices in a mesh: rep: 16 (over z, x, core), tp: 2 (over y).
Axes of the slice: x: 2, y: 2, z: 4, core: 2. Of those that a mesh axis runs over, the one named last changes fastest.
Arguments:
- tokens: bfloat16 [16, 256, 3072], P('rep', 'tp'), may hold values from -100 to 100
- norm_gain: float32 [16, 3072], P('rep'), may hold values from 0.5 to 1.5
- w_query: bfloat16 [16, 3072, 2048], P('rep', None, 'tp'), may hold values from -1 to 1
- key_weight: bfloat16 [16, 3072, 1024], P('rep', None, 'tp'), may hold values from -1 to 1
- value_weight: bfloat16 [16, 3072, 1024], P('rep', None, 'tp'), may hold values from -0.109375 to 0.109375
- attention_gradient: bfloat16 [16, 256, 2048], P('rep', None, 'tp'), may hold values from -6 to 6
- global_fragment: float32 [128, 3072], P('tp'), may hold values from -6 to 6
- momentum: float32 [128, 3072], P('tp'), may hold values from -3 to 3
- local_fragment: bfloat16 [16, 128, 3072], P('rep', 'tp'), may hold values from -6 to 6
Outputs:
- grad_query_w: bfloat16 [16, 3072, 2048], P('rep', None, 'tp')
- grad_key_w: bfloat16 [16, 3072, 1024], P('rep', None, 'tp')
- grad_value_w: bfloat16 [16, 3072, 1024], P('rep', None, 'tp')
- grad_gain: float32 [16, 3072], P('rep')
- grad_tokens: bfloat16 [16, 256, 3072], P('rep', 'tp')
- new_global: float32 [128, 3072], P('tp')
- new_momentum: float32 [128, 3072], P('tp')
All inputs are finite; a program needn't handle non-finite values.
Results may differ from a plain program's by a relative error of at most 0.019.
The roundings to bfloat16 on the way count: a program that leaves them out, or rounds other values in their place, can miss the bound.
Values may be sent and summed in bfloat16 or wider, within the bound.
No kernel may reach another device: no remote copies, remote signals or barrier semaphores. Data moves between devices by JAX's collectives and lax.ppermute only.
A program may use at most 128 MiB of HBM per device.

v0:
```python
import jax
import jax.numpy as jnp
from jax import lax
from jax.sharding import PartitionSpec as P

HEAD_SIZE = 128


epsilon = 1e-05
rope_base = 500000.0
outer_rate = 0.7
outer_momentum = 0.9


def rope_tables(sequence_length, width):
    middle = width // 2
    frequency = rope_base ** (-2.0 * jnp.arange(middle, dtype=jnp.float32) / width)
    angles = jnp.arange(sequence_length, dtype=jnp.float32)[:, None] * frequency[None, :]
    angles = jnp.concatenate([angles, angles], axis=1)
    return (jnp.cos(angles)[:, None, :], jnp.sin(angles)[:, None, :])


def rotate(vectors, cosine_table, sine_table):
    middle = vectors.shape[-1] // 2
    turned = jnp.concatenate([-vectors[..., middle:], vectors[..., :middle]], axis=-1)
    return vectors * cosine_table + turned * sine_table


def reverse_rotation(gradient, cosine_table, sine_table):
    middle = gradient.shape[-1] // 2
    shifted = gradient * sine_table
    turned = jnp.concatenate([shifted[..., middle:], -shifted[..., :middle]], axis=-1)
    return gradient * cosine_table + turned


def attention_reverse(query_rows, rotated_keys, values_bfloat, grad_out, block_of_rows):
    sequence_length = query_rows.shape[0]
    score_scale = query_rows.shape[-1] ** (-0.5)

    def one_block(running, block_index):
        acc_key, acc_value = running
        offset = block_index * block_of_rows
        query_block = lax.dynamic_slice_in_dim(query_rows, offset, block_of_rows, 0)
        grad_block = lax.dynamic_slice_in_dim(grad_out, offset, block_of_rows, 0)
        scores = (
            jnp.einsum(
                "qgrd,kgd->grqk", query_block, rotated_keys, preferred_element_type=jnp.float32
            )
            * score_scale
        )
        row_pos = offset + jnp.arange(block_of_rows)
        col_pos = jnp.arange(sequence_length)
        allowed = col_pos[None, :] <= row_pos[:, None]
        scores = jnp.where(allowed, scores, -jnp.inf)
        highest = jnp.max(scores, axis=-1, keepdims=True)
        powers = jnp.exp(scores - highest)
        probability = powers / jnp.sum(powers, axis=-1, keepdims=True)
        prob_low = probability.astype(jnp.bfloat16)
        acc_value = acc_value + jnp.einsum(
            "grqk,qgrd->kgd", prob_low, grad_block, preferred_element_type=jnp.float32
        )
        grad_prob = jnp.einsum(
            "qgrd,kgd->grqk", grad_block, values_bfloat, preferred_element_type=jnp.float32
        )
        grad_score = (
            probability
            * (grad_prob - jnp.sum(grad_prob * probability, axis=-1, keepdims=True))
            * score_scale
        )
        score_low = grad_score.astype(jnp.bfloat16)
        grad_query = jnp.einsum(
            "grqk,kgd->qgrd", score_low, rotated_keys, preferred_element_type=jnp.float32
        )
        acc_key = acc_key + jnp.einsum(
            "grqk,qgrd->kgd", score_low, query_block, preferred_element_type=jnp.float32
        )
        return ((acc_key, acc_value), grad_query)

    initial = jnp.zeros(rotated_keys.shape, jnp.float32)
    (acc_key, acc_value), grad_blocks = lax.scan(
        one_block, (initial, initial), jnp.arange(sequence_length // block_of_rows)
    )
    return (grad_blocks.reshape(query_rows.shape), acc_key, acc_value)


def body(
    tokens,
    norm_gain,
    w_query,
    key_weight,
    value_weight,
    attention_gradient,
    global_fragment,
    momentum,
    local_fragment,
):
    local_rows = tokens[0]
    norm_gains = norm_gain[0]
    weight_q = w_query[0]
    weight_k = key_weight[0]
    weight_v = value_weight[0]
    widened_rows = local_rows.astype(jnp.float32)
    inverse_norm = lax.rsqrt(
        jnp.mean(widened_rows * widened_rows, axis=-1, keepdims=True) + epsilon
    )
    normalized_input = widened_rows * inverse_norm
    normalized_local = (normalized_input * norm_gains[None, :]).astype(jnp.bfloat16)
    normalized = lax.all_gather(normalized_local, "tp", axis=0, tiled=True)
    sequence_length = normalized.shape[0]
    heads_q = weight_q.shape[1] // HEAD_SIZE
    heads_kv = weight_k.shape[1] // HEAD_SIZE
    cosine_table, sine_table = rope_tables(sequence_length, HEAD_SIZE)
    query_rows = jnp.dot(normalized, weight_q, preferred_element_type=jnp.float32).reshape(
        sequence_length, heads_q, HEAD_SIZE
    )
    query_rows = rotate(query_rows, cosine_table, sine_table).astype(jnp.bfloat16)
    rotated_keys = jnp.dot(normalized, weight_k, preferred_element_type=jnp.float32).reshape(
        sequence_length, heads_kv, HEAD_SIZE
    )
    rotated_keys = rotate(rotated_keys, cosine_table, sine_table).astype(jnp.bfloat16)
    values_bfloat = (
        jnp.dot(normalized, weight_v, preferred_element_type=jnp.float32)
        .astype(jnp.bfloat16)
        .reshape(sequence_length, heads_kv, HEAD_SIZE)
    )
    replica_group = heads_q // heads_kv
    block_of_rows = min(512, sequence_length)
    query_input_gradient, key_input_gradient, value_input_gradient = attention_reverse(
        query_rows.reshape(sequence_length, heads_kv, replica_group, HEAD_SIZE),
        rotated_keys,
        values_bfloat,
        attention_gradient[0].reshape(sequence_length, heads_kv, replica_group, HEAD_SIZE),
        block_of_rows,
    )
    dquery = (
        reverse_rotation(
            query_input_gradient.reshape(sequence_length, heads_q, HEAD_SIZE),
            cosine_table,
            sine_table,
        )
        .astype(jnp.bfloat16)
        .reshape(sequence_length, heads_q * HEAD_SIZE)
    )
    key_gradient = (
        reverse_rotation(key_input_gradient, cosine_table, sine_table)
        .astype(jnp.bfloat16)
        .reshape(sequence_length, heads_kv * HEAD_SIZE)
    )
    value_gradient = value_input_gradient.astype(jnp.bfloat16).reshape(
        sequence_length, heads_kv * HEAD_SIZE
    )
    contract = (((0,), (0,)), ((), ()))
    grad_wq = lax.dot_general(
        normalized, dquery, contract, preferred_element_type=jnp.float32
    ).astype(jnp.bfloat16)
    grad_wk = lax.dot_general(
        normalized, key_gradient, contract, preferred_element_type=jnp.float32
    ).astype(jnp.bfloat16)
    grad_wv = lax.dot_general(
        normalized, value_gradient, contract, preferred_element_type=jnp.float32
    ).astype(jnp.bfloat16)
    back = (((1,), (1,)), ((), ()))
    partial_value = lax.dot_general(dquery, weight_q, back, preferred_element_type=jnp.float32)
    partial_value = partial_value + lax.dot_general(
        key_gradient, weight_k, back, preferred_element_type=jnp.float32
    )
    summed_rows = lax.psum_scatter(
        (
            partial_value
            + lax.dot_general(value_gradient, weight_v, back, preferred_element_type=jnp.float32)
        ).astype(jnp.bfloat16),
        "tp",
        scatter_dimension=0,
        tiled=True,
    ).astype(jnp.float32)
    gains_gradient = lax.psum(jnp.sum(summed_rows * normalized_input, axis=0), "tp")
    scaled_rows = summed_rows * norm_gains[None, :]
    gradient_rows = (
        inverse_norm
        * (
            scaled_rows
            - normalized_input * jnp.mean(scaled_rows * normalized_input, axis=-1, keepdims=True)
        )
    ).astype(jnp.bfloat16)
    delta = global_fragment - local_fragment[0].astype(jnp.float32)
    replicas = lax.axis_size("rep")
    mean_delta = lax.psum(delta, "rep") / replicas
    new_momentum = outer_momentum * momentum + mean_delta
    new_global = global_fragment - outer_rate * (mean_delta + outer_momentum * new_momentum)
    return (
        grad_wq[None],
        grad_wk[None],
        grad_wv[None],
        gains_gradient[None],
        gradient_rows[None],
        new_global,
        new_momentum,
    )


def solution(mesh):
    placed = (
        P("rep", "tp", None),
        P("rep", None),
        P("rep", None, "tp"),
        P("rep", None, "tp"),
        P("rep", None, "tp"),
        P("rep", None, "tp"),
        P("tp", None),
        P("tp", None),
        P("rep", "tp", None),
    )
    return jax.shard_map(
        body,
        mesh=mesh,
        in_specs=placed,
        out_specs=(
            P("rep", None, "tp"),
            P("rep", None, "tp"),
            P("rep", None, "tp"),
            P("rep", None),
            P("rep", "tp", None),
            P("tp", None),
            P("tp", None),
        ),
        check_vma=False,
    )
```

profile of v0, /device:TPU:0, one launch (start us, length us, event | category | flops | bytes accessed | tf_op | source)
XLA Modules:
  0.0 146.9 jit_solution(9005998716346742518)
XLA Ops:
  8.0 0.0 all-gather.2.cloned.1.call-start
  8.1 1.6 %fusion.25 = f32[128]{0:T(128)S(1)} fusion(bf16[1,128,3072]{2,1,0:T(8,128)(2,1)} %param.9), kind=kLoop, calls=%fused_computation.37 | loop fusion | flops 1179520 | bytes 786944 | tf_op jit(solution)/shard_map/reduce_sum | solution.py:104
  9.6 2.3 %fusion.22 = bf16[128,3072]{1,0:T(8,128)(2,1)} fusion(bf16[1,128,3072]{2,1,0:T(8,128)(2,1)} %param.9, f32[3072]{0:T(1024)} %bitcast.153, f32[128]{0:T(128)S(1)} %add_rsqrt_fusion), kind=kLoop, calls=%fused_computation.34 | loop fusion | flops 1572864 | bytes 1585664 | tf_op jit(solution)/shard_map/convert_element_type | solution.py:107
  11.9 0.0 all-gather.2.cloned.1.call-update
  11.9 0.0 all-reduce.2.cloned.1.call-start
  12.0 2.1 %convert_subtract_fusion = f32[64,3072]{1,0:T(8,128)} fusion(f32[64,3072]{1,0:T(8,128)} %param.15, bf16[1,64,3072]{2,1,0:T(8,128)(2,1)S(1)} %copy-done.19), kind=kLoop, calls=%fused_computation.65 | loop fusion | flops 393216 | bytes 1966080 | tf_op jit(solution)/shard_map/sub | solution.py:185
  14.1 0.0 all-reduce.2.cloned.1.call-update
  14.1 0.0 reduce-scatter.2.cloned.1.call-start
  14.2 8.7 %copy.38 = bf16[1024,3072]{1,0:T(8,128)(2,1)} copy(bf16[1024,3072]{0,1:T(8,128)(2,1)} %bitcast.138) | data formatting | bytes 12582912 | tf_op jit(solution)/shard_map/dot_general | solution.py:113
  22.9 0.1 iota_multiply_fusion
  23.0 0.5 fusion.56
  23.4 4.7 %copy.35 = bf16[512,3072]{1,0:T(8,128)(2,1)} copy(bf16[512,3072]{0,1:T(8,128)(2,1)} %bitcast.137) | data formatting | bytes 6291456 | tf_op jit(solution)/shard_map/dot_general | solution.py:117
  28.1 2.0 %copy.41 = bf16[1,256,1024]{1,2,0:T(8,128)(2,1)} copy(bf16[1,256,1024]{2,1,0:T(8,128)(2,1)} %param.14) | data formatting | bytes 1048576 | tf_op jit(solution)/shard_map/reshape;squeeze | solution.py:132
  30.2 11.8 %all-gather.2.cloned.1.call-done = bf16[256,3072]{1,0:T(8,128)(2,1)} async-done(((bf16[128,3072]{1,0:T(8,128)(2,1)}), bf16[256,3072]{1,0:T(8,128)(2,1)}) %all-gather.2.cloned.1.call-update) | async-done | bytes 1572880 | tf_op jit(solution)/shard_map/all_gather | solution.py:108
  42.0 5.3 %fusion.26 = f32[256,8,128]{0,2,1:T(8,128)S(1)} fusion(bf16[8,128,3072]{2,1,0:T(8,128)(2,1)} %bitcast.141, bf16[256,3072]{1,0:T(8,128)(2,1)} %all-gather.2.cloned.1.call-done), kind=kOutput, calls=%fused_computation.38 | convolution fusion | flops 1610612736 | bytes 8912896 | tf_op jit(solution)/shard_map/dot_general | solution.py:113
  47.3 1.1 slice_negate_fusion.1
  48.4 1.1 copy-done.1
  49.5 1.1 fusion.28
  50.5 0.9 slice_negate_fusion.3
  51.5 0.0 copy-done.9
  51.5 1.7 %fusion.30 = bf16[256,512]{1,0:T(8,128)(2,1)} fusion(bf16[256,3072]{1,0:T(8,128)(2,1)S(1)} %copy-done.1, bf16[1,3072,512]{2,1,0:T(8,128)(2,1)S(1)} %copy-done), kind=kOutput, calls=%fused_computation.44 | convolution fusion | flops 805437440 | bytes 4980736 | tf_op jit(solution)/shard_map/dot_general | solution.py:122
  53.2 1.7 %reshape.115 = bf16[256,4,128]{2,1,0:T(4,128)(2,1)} reshape(bf16[256,512]{1,0:T(8,128)(2,1)} %fusion.30) | data formatting | bytes 524288 | tf_op jit(solution)/shard_map/reshape | solution.py:124
  55.0 2.7 %fusion.35 = bf16[256,8,128]{0,2,1:T(8,128)(2,1)} fusion(f32[256,8,64]{0,2,1:T(8,128)} %get-tuple-element.40, f32[256,8,64]{0,2,1:T(8,128)} %get-tuple-element.39, f32[256,8,128]{0,2,1:T(8,128)} %copy-done.7, f32[256,128]{0,1:T(8,128)S(1)} %get-tuple-element.46, f32[256,128]{0,1:T(8,128)S(1)} %get-tuple-element.45), kind=kLoop, calls=%fused_computation.48 | loop fusion | flops 1310720 | bytes 2883584 | tf_op jit(solution)/shard_map/convert_element_type | solution.py:116
  57.7 0.8 fusion.50
  58.5 1.7 %fusion.51 = f32[4,256,256,2]{2,1,3,0:T(8,128)} fusion(bf16[256,4,2,128]{0,3,2,1:T(8,128)(2,1)S(1)} %bitcast.146, bf16[256,4,128,1]{2,1,0,3:T(4,128)(2,1)S(1)} %bitcast.149), kind=kOutput, calls=%fused_computation.78 | convolution fusion | flops 134217728 | bytes 2883584 | tf_op jit(solution)/shard_map/while/body/eval_jaxpr/qgrd,kgd->grqk/dot_general | solution.py:62
  60.2 3.3 %fusion.65 = (f32[4,2,256]{2,1,0:T(2,128)S(1)}, f32[4,2,256,256]{2,3,1,0:T(8,128)}) fusion(pred[256,256]{0,1:T(8,128)(4,1)S(1)} %iota_compare_fusion, bf16[256,4,128,1]{0,2,3,1:T(8,128)(2,1)} %fusion.50, bf16[256,4,2,128]{0,3,2,1:T(8,128)(2,1)} %bitcast.150), kind=kOutput, calls=%fused_computation.98 | convolution fusion | flops 136315136 | bytes 2957312 | tf_op jit(solution)/shard_map/while/body/eval_jaxpr/sub | solution.py:56
  63.5 5.4 %broadcast_multiply_fusion = (f32[256,4,128]{0,2,1:T(8,128)}, f32[256,4,128]{0,2,1:T(8,128)}) fusion(f32[256,128]{0,1:T(8,128)S(1)} %get-tuple-element.46, bf16[256,4,2,128]{0,3,2,1:T(8,128)(2,1)} %bitcast.151, f32[4,256,256,2]{2,1,3,0:T(8,128)} %fusion.51, f32[4,2,256,256]{2,3,1,0:T(8,128)} %get-tuple-element.48, f32[4,2,256]{2,1,0:T(2,128)S(1)} %get-tuple-element.47), kind=kOutput, calls=%fused_computation.81 | convolution fusion | flops 138021120 | bytes 5906432 | tf_op jit(solution)/shard_map/while/body/eval_jaxpr/grqk,qgrd->kgd/dot_general | solution.py:74
  68.8 5.3 %fusion.44 = f32[4,128,2,256]{3,1,2,0:T(8,128)} fusion(bf16[256,4,128,1]{0,2,3,1:T(8,128)(2,1)} %fusion.50, f32[4,256,256,2]{2,1,3,0:T(8,128)} %fusion.51, f32[4,2,256,256]{2,3,1,0:T(8,128)} %get-tuple-element.48, f32[4,2,256]{2,1,0:T(2,128)S(1)} %get-tuple-element.47), kind=kOutput, calls=%fused_computation.62 | convolution fusion | flops 137890048 | bytes 5513216 | tf_op jit(solution)/shard_map/while/body/eval_jaxpr/grqk,kgd->qgrd/dot_general | solution.py:71
  74.2 2.3 %fusion.33 = bf16[4,256,128]{1,2,0:T(8,128)(2,1)S(1)} fusion(bf16[256,4,2,128]{0,3,2,1:T(8,128)(2,1)} %bitcast.145, f32[4,2,256,256]{2,3,1,0:T(8,128)} %get-tuple-element.48, f32[4,2,256]{2,1,0:T(2,128)S(1)} %get-tuple-element.47), kind=kOutput, calls=%fused_computation.45 | convolution fusion | flops 135397376 | bytes 2891776 | tf_op jit(solution)/shard_map/while/body/eval_jaxpr/grqk,qgrd->kgd/dot_general | solution.py:59
  76.6 0.1 bitcast_multiply_fusion.3
  76.7 0.1 fusion.63
  76.7 1.1 fusion.39
  77.9 1.1 slice-done.1
  79.0 1.8 %fusion.2 = f32[256,3072]{1,0:T(8,128)S(1)} fusion(bf16[256,1024]{0,1:T(8,128)(2,1)S(1)} %bitcast.152, bf16[1,3072,1024]{2,1,0:T(8,128)(2,1)S(1)} %bitcast.140), kind=kOutput, calls=%fused_computation.2 | convolution fusion | flops 1610612736 | bytes 9961472 | tf_op jit(solution)/shard_map/dot_general | solution.py:163
  80.8 0.1 fusion.49
  80.9 0.1 copy-done.3
  81.0 1.1 convolution_add_fusion.1
  82.1 2.2 %fusion.6 = bf16[256,3072]{1,0:T(8,128)(2,1)} fusion(f32[256,3072]{1,0:T(8,128)S(1)} %convolution_add_fusion.1, bf16[256,512]{0,1:T(8,128)(2,1)S(1)} %bitcast.147, bf16[1,3072,512]{2,1,0:T(8,128)(2,1)S(1)} %copy-done), kind=kOutput, calls=%fused_computation.11 | convolution fusion | flops 806879232 | bytes 8126464 | tf_op jit(solution)/shard_map/dot_general | solution.py:170
  84.3 27.0 %all-reduce.2.cloned.1.call-done = f32[64,3072]{1,0:T(8,128)} async-done(((f32[64,3072]{1,0:T(8,128)}), f32[64,3072]{1,0:T(8,128)}) %all-reduce.2.cloned.1.call-update) | async-done | bytes 786448 | tf_op jit(solution)/shard_map/psum | solution.py:187
  111.3 3.1 %multiply_subtract_fusion = (f32[64,3072]{1,0:T(8,128)}, f32[64,3072]{1,0:T(8,128)}) fusion(f32[64,3072]{1,0:T(8,128)} %param.15, f32[64,3072]{1,0:T(8,128)} %all-reduce.2.cloned.1.call-done, f32[64,3072]{1,0:T(8,128)} %param.16), kind=kLoop, calls=%fused_computation.66 | loop fusion | flops 1376256 | bytes 3932160 | tf_op jit(solution)/shard_map/sub | solution.py:189
  114.5 0.2 fusion.37
  114.7 1.2 copy-done.2
  115.9 2.9 %fusion.5 = bf16[1,3072,512]{2,1,0:T(8,128)(2,1)} fusion(bf16[256,3072]{1,0:T(8,128)(2,1)S(1)} %copy-done.2, bf16[256,512]{0,1:T(8,128)(2,1)S(1)} %bitcast.148), kind=kOutput, calls=%fused_computation.8 | convolution fusion | flops 806879232 | bytes 4980736 | tf_op jit(solution)/shard_map/dot_general | solution.py:159
  118.8 2.7 %fusion.4 = bf16[1,3072,512]{2,1,0:T(8,128)(2,1)} fusion(bf16[256,3072]{1,0:T(8,128)(2,1)S(1)} %copy-done.2, bf16[256,512]{0,1:T(8,128)(2,1)S(1)} %bitcast.144), kind=kOutput, calls=%fused_computation.7 | convolution fusion | flops 806879232 | bytes 4980736 | tf_op jit(solution)/shard_map/dot_general | solution.py:156
  121.5 4.6 %convert_bitcast_fusion = bf16[1,3072,1024]{2,1,0:T(8,128)(2,1)} fusion(bf16[256,3072]{1,0:T(8,128)(2,1)S(1)} %copy-done.2, bf16[256,1024]{0,1:T(8,128)(2,1)S(1)} %fusion.37), kind=kOutput, calls=%fused_computation.4 | convolution fusion | flops 1613758464 | bytes 8388608 | tf_op jit(solution)/shard_map/dot_general | solution.py:153
  126.1 1.9 %fusion.24 = (f32[128]{0:T(128)S(1)}, f32[3072]{0:T(1024)S(1)}) fusion(bf16[128,3072]{1,0:T(8,128)(2,1)} %reduce-scatter.2.cloned.1.call-done, bf16[1,128,3072]{2,1,0:T(8,128)(2,1)} %param.9, f32[3072]{0:T(1024)S(1)} %bitcast.154, f32[128]{0:T(128)S(1)} %add_rsqrt_fusion), kind=kLoop, calls=%fused_computation.36 | loop fusion | flops 3142528 | bytes 1598464 | tf_op jit(solution)/shard_map/reduce_sum | solution.py:182
  128.0 8.8 %psum.14 = f32[1,3072]{1,0:T(1,128)} all-reduce(f32[1,3072]{1,0:T(1,128)S(1)} %bitcast.156), channel_id=1, replica_groups=mesh['rep'=16,'tp'=2] {'tp'}, use_global_device_ids=true, to_apply=%region_6.7 | all-reduce | flops 3072 | bytes 24576 | tf_op jit(solution)/shard_map/psum | solution.py:176
  136.8 2.7 %fusion.46 = bf16[1,128,3072]{2,1,0:T(8,128)(2,1)} fusion(bf16[128,3072]{1,0:T(8,128)(2,1)} %reduce-scatter.2.cloned.1.call-done, bf16[1,128,3072]{2,1,0:T(8,128)(2,1)} %param.9, f32[128]{0:T(128)S(1)} %broadcast_multiply_fusion.1, f32[3072]{0:T(1024)S(1)} %bitcast.155, f32[128]{0:T(128)S(1)} %add_rsqrt_fusion), kind=kLoop, calls=%fused_computation.64 | loop fusion | flops 3145728 | bytes 2372608 | tf_op jit(solution)/shard_map/broadcast_in_dim | solution.py:195
  (49 shorter events, 0.2 us)
Async XLA Ops:
  8.0 43.5 %copy-start = (bf16[1,3072,512]{2,1,0:T(8,128)(2,1)S(1)}, bf16[1,3072,512]{2,1,0:T(8,128)(2,1)}, u32[]{:S(2)}) copy-start(bf16[1,3072,512]{2,1,0:T(8,128)(2,1)} %param.13) | copy-start | bytes 9437188
  8.0 4.0 %copy-start.19 = (bf16[1,64,3072]{2,1,0:T(8,128)(2,1)S(1)}, bf16[1,64,3072]{2,1,0:T(8,128)(2,1)}, u32[]{:S(2)}) copy-start(bf16[1,64,3072]{2,1,0:T(8,128)(2,1)} %param.17) | copy-start | bytes 1179652
  8.0 34.0 %all-gather.2.cloned.1.call-start = ((), (), s32[]{:S(2)}) async-start(), calls=%async_computation.1 | async-start | bytes 2359296 | tf_op jit(solution)/shard_map/all_gather | solution.py:108
  11.9 99.4 %all-reduce.2.cloned.1.call-start = ((), (), s32[]{:S(2)}) async-start(), calls=%async_computation.3 | async-start | bytes 1572864 | tf_op jit(solution)/shard_map/psum | solution.py:187
  14.1 112.0 %reduce-scatter.2.cloned.1.call-start = ((), (), s32[]{:S(2)}) async-start(), calls=%async_computation.2 | async-start | bytes 2359296 | tf_op jit(solution)/shard_map/reduce_scatter | solution.py:167
  42.0 6.4 %copy-start.8 = (bf16[512,3072]{1,0:T(8,128)(2,1)S(1)}, bf16[512,3072]{1,0:T(8,128)(2,1)}, u32[]{:S(2)}) copy-start(bf16[512,3072]{1,0:T(8,128)(2,1)} %copy.35) | copy-start | bytes 9437188
  47.3 3.2 %copy-start.7 = (f32[256,8,128]{0,2,1:T(8,128)}, f32[256,8,128]{0,2,1:T(8,128)S(1)}, u32[]{:S(2)}) copy-start(f32[256,8,128]{0,2,1:T(8,128)S(1)} %fusion.26) | copy-start | bytes 3145732
  47.3 2.2 %copy-start.1 = (bf16[256,3072]{1,0:T(8,128)(2,1)S(1)}, bf16[256,3072]{1,0:T(8,128)(2,1)}, u32[]{:S(2)}) copy-start(bf16[256,3072]{1,0:T(8,128)(2,1)} %all-gather.2.cloned.1.call-done) | copy-start | bytes 4718596
  50.5 1.0 copy-start.9
  55.0 2.7 %copy-start.10 = (f32[256,4,128]{0,2,1:T(8,128)S(1)}, f32[256,4,128]{0,2,1:T(8,128)}, u32[]{:S(2)}) copy-start(f32[256,4,128]{0,2,1:T(8,128)} %copy-done.9) | copy-start | bytes 1572868
  55.0 2.7 %copy-start.14 = (f32[256,4,64]{0,2,1:T(8,128)S(1)}, f32[256,4,64]{0,2,1:T(8,128)}, u32[]{:S(2)}) copy-start(f32[256,4,64]{0,2,1:T(8,128)} %get-tuple-element.43) | copy-start | bytes 786436
  55.0 2.7 %copy-start.15 = (f32[256,4,64]{0,2,1:T(8,128)S(1)}, f32[256,4,64]{0,2,1:T(8,128)}, u32[]{:S(2)}) copy-start(f32[256,4,64]{0,2,1:T(8,128)} %get-tuple-element.44) | copy-start | bytes 786436
  55.0 3.5 %copy-start.11 = (bf16[1,256,1024]{1,2,0:T(8,128)(2,1)S(1)}, bf16[1,256,1024]{1,2,0:T(8,128)(2,1)}, u32[]{:S(2)}) copy-start(bf16[1,256,1024]{1,2,0:T(8,128)(2,1)} %copy.41) | copy-start | bytes 1572868
  55.0 3.5 %copy-start.16 = (bf16[256,4,128]{2,1,0:T(4,128)(2,1)S(1)}, bf16[256,4,128]{2,1,0:T(4,128)(2,1)}, u32[]{:S(2)}) copy-start(bf16[256,4,128]{2,1,0:T(4,128)(2,1)} %reshape.115) | copy-start | bytes 786436
  74.2 2.3 %copy-start.17 = (f32[256,4,128]{0,2,1:T(8,128)S(1)}, f32[256,4,128]{0,2,1:T(8,128)}, u32[]{:S(2)}) copy-start(f32[256,4,128]{0,2,1:T(8,128)} %get-tuple-element.49) | copy-start | bytes 1572868
  74.2 2.4 %copy-start.4 = (f32[4,128,2,256]{3,1,2,0:T(8,128)S(1)}, f32[4,128,2,256]{3,1,2,0:T(8,128)}, u32[]{:S(2)}) copy-start(f32[4,128,2,256]{3,1,2,0:T(8,128)} %fusion.44) | copy-start | bytes 3145732
  74.2 3.7 %slice-start = ((s8[6291456]{0:T(1024)(128)(4,1)}), s8[4194304]{0:T(1024)(128)(4,1)S(1)}, s32[]{:S(2)}) async-start(s8[6291456]{0:T(1024)(128)(4,1)} %bitcast.139), calls=%async_computation.4 | async-start | bytes 8388608
  76.5 5.6 %copy-start.12 = (bf16[4,256,128]{1,2,0:T(8,128)(2,1)}, bf16[4,256,128]{1,2,0:T(8,128)(2,1)S(1)}, u32[]{:S(2)}) copy-start(bf16[4,256,128]{1,2,0:T(8,128)(2,1)S(1)} %fusion.33) | copy-start | bytes 786436
  76.5 2.5 %slice-start.1 = ((s8[6291456]{0:T(1024)(128)(4,1)}), s8[2097152]{0:T(1024)(128)(4,1)S(1)}, s32[]{:S(2)}) async-start(s8[6291456]{0:T(1024)(128)(4,1)} %bitcast.139), calls=%async_computation.5 | async-start | bytes 4194304
  79.0 1.9 %copy-start.18 = (f32[256,4,128]{0,2,1:T(8,128)S(1)}, f32[256,4,128]{0,2,1:T(8,128)}, u32[]{:S(2)}) copy-start(f32[256,4,128]{0,2,1:T(8,128)} %get-tuple-element.50) | copy-start | bytes 1572868
  79.0 2.1 %copy-start.3 = (bf16[1,3072,512]{2,1,0:T(8,128)(2,1)S(1)}, bf16[1,3072,512]{2,1,0:T(8,128)(2,1)}, u32[]{:S(2)}) copy-start(bf16[1,3072,512]{2,1,0:T(8,128)(2,1)} %param.12) | copy-start | bytes 9437188
  111.3 3.1 %copy-start.5 = (f32[4,128,2,256]{3,1,2,0:T(8,128)S(1)}, f32[4,128,2,256]{3,1,2,0:T(8,128)}, u32[]{:S(2)}) copy-start(f32[4,128,2,256]{3,1,2,0:T(8,128)} %fusion.44) | copy-start | bytes 3145732
  111.3 3.1 %copy-start.6 = (f32[256,8,128]{0,2,1:T(8,128)S(1)}, f32[256,8,128]{0,2,1:T(8,128)}, u32[]{:S(2)}) copy-start(f32[256,8,128]{0,2,1:T(8,128)} %get-tuple-element.36) | copy-start | bytes 3145732
  114.5 1.4 copy-start.2
  114.5 1.4 copy-start.13
  121.5 4.6 %copy-start.20 = (f32[1,3072]{1,0:T(1,128)S(1)}, f32[1,3072]{1,0:T(1,128)}, u32[]{:S(2)}) copy-start(f32[1,3072]{1,0:T(1,128)} %param.10) | copy-start | bytes 36868
Sparse Core Ops, SparseCore 0:
  12.1 29.9 all-gather.1
  84.5 26.1 reduce-scatter.1
Sparse Core Ops, SparseCore 1:
  16.4 94.9 all-reduce.1
where the time goes:
time: 148 us; the launch traced here: 147 us
  matrix products  41.3 us (28%)
  waiting for transfers between devices  38.9 us (26%)
  other arithmetic  21.3 us (14%)
  local copies, waits for them, and re-layouts  20.8 us (14%)
  between operations  15.7 us (11%)
  blocking collectives  8.76 us (6%)
    psum x1, waiting for transfers between devices, body(): mean_delta = lax.psum(delta, 'rep') / replicas  27 us
    all_gather x1, waiting for transfers between devices, body(): normalized = lax.all_gather(normalized_local, 'tp', axis=0, tiled=True)  11.8 us
    psum x1, blocking collectives, body(): lax.psum(jnp.sum(summed_rows * normalized_input, axis=0), 'tp')  8.76 us
    dot_general x1, local copies, waits for them, and re-layouts, body(): jnp.dot(normalized, weight_q, preferred_element_type=jnp.float32)  8.68 us
    dot_general x1, matrix products, one_block(): jnp.einsum('grqk,qgrd->kgd', score_low, query_block, preferred_element_ty...  5.36 us
    dot_general x1, matrix products, one_block(): jnp.einsum('grqk,kgd->qgrd', score_low, rotated_keys, preferred_element_t...  5.3 us
    dot_general x1, matrix products, body(): jnp.dot(normalized, weight_q, preferred_element_type=jnp.float32)  5.26 us
    dot_general x1, local copies, waits for them, and re-layouts, body(): jnp.dot(normalized, weight_k, preferred_element_type=jnp.float32)  4.69 us
  transfers between devices with their start and end apart: 3, of which 2 were waited for; matrix products, arithmetic and copies ran while one was open for 49% of the time, Pallas kernels for 0%

commit v1 on v0

v1 whole, which is shorter than its diff:
```python
import functools

import jax
import jax.numpy as jnp
import numpy as np
from jax import lax
from jax.experimental import pallas as pl
from jax.experimental.pallas import tpu as pltpu
from jax.sharding import PartitionSpec as P


HEAD_SIZE = 128

epsilon = 1e-05
rope_base = 500000.0
outer_rate = 0.7
outer_momentum = 0.9

VMEM = pltpu.VMEM
f32, bf16 = jnp.float32, jnp.bfloat16

MAX_CHUNKS = 2
WEIGHT_ROWS = 768


def whole():
    return pl.BlockSpec(memory_space=VMEM)


def anywhere():
    return pl.BlockSpec(memory_space=pl.ANY)


def far(array):
    return pltpu.with_memory_space_constraint(array, pltpu.HBM)


def smem():
    return pl.BlockSpec(memory_space=pltpu.SMEM)


def params(mib):
    return pltpu.CompilerParams(vmem_limit_bytes=mib << 20)


def cost(flops, nbytes):
    return pl.CostEstimate(flops=int(flops), bytes_accessed=int(nbytes), transcendentals=0)


def rope_tables(length, width):
    middle = width // 2
    frequency = rope_base ** (-2.0 * np.arange(middle) / width)
    angles = np.arange(length)[:, None] * frequency[None, :]
    cosine, sine = np.cos(angles), np.sin(angles)
    tables = (cosine, cosine, -sine, sine)
    return jnp.asarray(np.concatenate(tables, 1).astype(np.float32))


def rope(v, cosine, sine):
    return v * cosine + pltpu.roll(v, v.shape[-1] // 2, 1) * sine


def unrope(v, cosine, sine):
    return v * cosine - pltpu.roll(v, v.shape[-1] // 2, 1) * sine


def chunk_count(width):
    for n in range(MAX_CHUNKS, 1, -1):
        if width % (n * 128) == 0:
            return n
    return 1


def step_size(width, most):
    for n in range(most, 0, -128):
        if width % n == 0:
            return n
    return width


def norm_kernel(x_ref, gain_ref, *outs):
    x = x_ref[...].astype(f32)
    inverse = lax.rsqrt(jnp.mean(x * x, axis=-1, keepdims=True) + epsilon)
    normed = ((x * inverse) * gain_ref[...]).astype(bf16)
    width = outs[0].shape[1]
    for c, out in enumerate(outs):
        out[...] = normed[:, c * width : (c + 1) * width]


def norm(x, gain, chunks):
    rows, width = x.shape
    return pl.pallas_call(
        norm_kernel,
        out_shape=[jax.ShapeDtypeStruct((rows, width // chunks), bf16)] * chunks,
        in_specs=[whole()] * 2,
        out_specs=[whole()] * chunks,
        compiler_params=params(8),
        cost_estimate=cost(1.0e9, x.size * 4),
        name="norm",
    )(far(x), far(gain))


def project(chunk, wq, wk, wv, rows):
    return [jnp.dot(chunk, w[rows, :], preferred_element_type=f32) for w in (wq, wk, wv)]


def finish_projection(parts, tables, out, row):
    rows = tables.shape[0]
    cosine, sine = tables[:, :HEAD_SIZE], tables[:, HEAD_SIZE:]
    at = 0
    for part, turned in zip(parts, (True, True, False)):
        for h in range(part.shape[1] // HEAD_SIZE):
            piece = part[:, h * HEAD_SIZE : (h + 1) * HEAD_SIZE]
            if turned:
                piece = rope(piece, cosine, sine)
            out[pl.ds(row, rows), at : at + HEAD_SIZE] = piece.astype(bf16)
            at += HEAD_SIZE


def keep(chunk, normed_all, row, part, sem):
    rows, width = chunk.shape
    place = normed_all.at[pl.ds(row, rows), pl.ds(part * width, width)]
    copy = pltpu.make_async_copy(chunk, place, sem)
    copy.start()
    return copy


def own_kernel(block, depth, index_ref, tables, *refs):
    chunks = refs[:-11]
    wq, wk, wv, out, normed_all, bq, bk, bv, acc, sems, keep_sems = refs[-11:]
    rows, width = chunks[0].shape
    start = pl.multiple_of(index_ref[0] * rows, rows)
    steps = wq.shape[0] // block
    sources, buffers = (wq, wk, wv), (bq, bk, bv)

    def fetch(s):
        part = pl.ds(s * block, block)
        copies = [
            pltpu.make_async_copy(sources[i].at[part], buffers[i].at[part], sems.at[s * 3 + i])
            for i in range(3)
        ]
        for copy in copies:
            copy.start()
        return copies

    flights = [fetch(s) for s in range(depth)]
    kept = [keep(ref, normed_all, start, c, keep_sems.at[c]) for c, ref in enumerate(chunks)]
    for s in range(steps):
        for copy in flights[s]:
            copy.wait()
        if s + depth < steps:
            flights.append(fetch(s + depth))
        c, at = divmod(s * block, width)
        parts = project(chunks[c][:, at : at + block], bq, bk, bv, slice(s * block, (s + 1) * block))
        at = 0
        for part in parts:
            cols = slice(at, at + part.shape[1])
            if s == 0:
                acc[:, cols] = part
            else:
                acc[:, cols] += part
            at += part.shape[1]
    qc, kc = wq.shape[1], wk.shape[1]
    parts = acc[:, :qc], acc[:, qc : qc + kc], acc[:, qc + kc :]
    finish_projection(parts, tables[pl.ds(start, rows), :], out, 0)
    for copy in kept:
        copy.wait()


def project_own(index, chunks, wq, wk, wv, tables):
    rows, width = chunks[0].shape
    qc, kc = wq.shape[1], wk.shape[1]
    block = step_size(width, 512)
    full = wq.shape[0]
    steps = full // block
    total = qc + 2 * kc
    return pl.pallas_call(
        functools.partial(own_kernel, block, min(3, steps)),
        out_shape=[
            jax.ShapeDtypeStruct((rows, total), bf16),
            jax.ShapeDtypeStruct((tables.shape[0], full), bf16),
        ],
        in_specs=[smem(), whole()] + [whole()] * len(chunks) + [anywhere()] * 3,
        out_specs=[whole(), anywhere()],
        scratch_shapes=[
            VMEM((full, qc), bf16),
            VMEM((full, kc), bf16),
            VMEM((full, kc), bf16),
            VMEM((rows, total), f32),
            pltpu.SemaphoreType.DMA((steps * 3,)),
            pltpu.SemaphoreType.DMA((len(chunks),)),
        ],
        compiler_params=params(20),
        cost_estimate=cost(5e9, full * total * 2),
        name="own_projection",
    )(index, tables, *chunks, *[far(w) for w in (wq, wk, wv)])


def part_kernel(part, row_ref, chunk, wq, wk, wv, *rest):
    out, normed_all, sem = rest[-3:]
    acc_in = rest[0] if len(rest) > 4 else None
    rows, width = chunk.shape
    kept = keep(chunk, normed_all, pl.multiple_of(row_ref[0] * rows, rows), part, sem)
    at = 0
    for value in project(chunk[...], wq, wk, wv, slice(part * width, (part + 1) * width)):
        cols = slice(at, at + value.shape[1])
        out[:, cols] = value if acc_in is None else acc_in[:, cols] + value
        at += value.shape[1]
    kept.wait()


def project_part(owner, chunk, wq, wk, wv, acc, normed_all, part):
    rows, width = chunk.shape
    total = wq.shape[1] + 2 * wk.shape[1]
    extra = [] if acc is None else [acc]
    inputs = 5 + len(extra)
    return pl.pallas_call(
        functools.partial(part_kernel, part),
        out_shape=[
            jax.ShapeDtypeStruct((rows, total), f32),
            jax.ShapeDtypeStruct(normed_all.shape, bf16),
        ],
        in_specs=[smem()] + [whole()] * (4 + len(extra)) + [anywhere()],
        out_specs=[whole(), anywhere()],
        input_output_aliases={inputs: 1},
        scratch_shapes=[pltpu.SemaphoreType.DMA],
        compiler_params=params(20),
        cost_estimate=cost(2 * rows * width * total, width * total * 2),
        name="part_projection",
    )(owner, chunk, wq, wk, wv, *extra, far(normed_all))


def attention(all_rows, grad_out, tables, out, qc, kc, block):
    length = all_rows.shape[0]
    group = qc // kc
    scale = HEAD_SIZE ** (-0.5)
    nt = (((1,), (1,)), ((), ()))
    tn = (((0,), (0,)), ((), ()))
    key = lax.broadcasted_iota(jnp.int32, (block, block), 0)
    query = lax.broadcasted_iota(jnp.int32, (block, block), 1)
    allowed = jnp.concatenate([key <= query] * group, 1)
    blocks = length // block
    for g in range(kc // HEAD_SIZE):
        kcols = slice(qc + g * HEAD_SIZE, qc + (g + 1) * HEAD_SIZE)
        vcols = slice(qc + kc + g * HEAD_SIZE, qc + kc + (g + 1) * HEAD_SIZE)
        dk = [None] * blocks
        dv = [None] * blocks
        for a in range(blocks):
            rows = slice(a * block, (a + 1) * block)
            keys = (a + 1) * block
            head = lambda r: slice((g * group + r) * HEAD_SIZE, (g * group + r + 1) * HEAD_SIZE)
            q = jnp.concatenate([all_rows[rows, head(r)] for r in range(group)], 0)
            do = jnp.concatenate([grad_out[rows, head(r)] for r in range(group)], 0)
            k = all_rows[:keys, kcols]
            v = all_rows[:keys, vcols]
            s = lax.dot_general(k, q, nt, preferred_element_type=f32) * scale
            corner = jnp.where(allowed, s[keys - block :], -jnp.inf)
            s = corner if a == 0 else jnp.concatenate([s[: keys - block], corner], 0)
            gprob = lax.dot_general(v, do, nt, preferred_element_type=f32)
            powers = jnp.exp(s - jnp.max(s, axis=0, keepdims=True))
            prob = powers * (1.0 / jnp.sum(powers, axis=0, keepdims=True))
            inner = jnp.sum(gprob * prob, axis=0, keepdims=True)
            low = prob.astype(bf16)
            ds = (prob * (gprob - inner) * scale).astype(bf16)
            part_v = jnp.dot(low, do, preferred_element_type=f32)
            part_k = jnp.dot(ds, q, preferred_element_type=f32)
            dq = lax.dot_general(k, ds, tn, preferred_element_type=f32).T
            for b in range(a + 1):
                piece = slice(b * block, (b + 1) * block)
                dv[b] = part_v[piece] if dv[b] is None else dv[b] + part_v[piece]
                dk[b] = part_k[piece] if dk[b] is None else dk[b] + part_k[piece]
            cosine, sine = tables[rows, :HEAD_SIZE], tables[rows, HEAD_SIZE:]
            for r in range(group):
                piece = unrope(dq[r * block : (r + 1) * block], cosine, sine)
                out[rows, head(r)] = piece.astype(bf16)
        for b in range(blocks):
            rows = slice(b * block, (b + 1) * block)
            cosine, sine = tables[rows, :HEAD_SIZE], tables[rows, HEAD_SIZE:]
            out[rows, kcols] = unrope(dk[b], cosine, sine).astype(bf16)
            out[rows, vcols] = dv[b].astype(bf16)


def last_kernel(part, others, index_ref, chunk, wq, wk, wv, *rest):
    acc_in = rest[0] if len(rest) > others + 7 else None
    ready = rest[-(others + 7) : -7]
    grad_out, tables, _, out, normed_all, all_rows, sem = rest[-7:]
    rows, width = chunk.shape
    qc, kc = wq.shape[1], wk.shape[1]
    n = others + 1
    start = pl.multiple_of(lax.rem(index_ref[0] + 1, n) * rows, rows)
    kept = keep(chunk, normed_all, start, part, sem)
    for d, ref in enumerate(ready):
        owner = lax.rem(index_ref[0] + (n - d), n)
        all_rows[pl.ds(pl.multiple_of(owner * rows, rows), rows), :] = ref[...]
    parts = project(chunk[...], wq, wk, wv, slice(part * width, (part + 1) * width))
    if acc_in is not None:
        before = acc_in[:, :qc], acc_in[:, qc : qc + kc], acc_in[:, qc + kc :]
        parts = [b + p for b, p in zip(before, parts)]
    finish_projection(parts, tables[pl.ds(start, rows), :], all_rows, start)
    attention(all_rows, grad_out, tables, out, qc, kc, rows)
    kept.wait()


def last_and_attention(index, chunk, wq, wk, wv, acc, ready, grad_out, tables, normed_all, part):
    _, width = chunk.shape
    total = wq.shape[1] + 2 * wk.shape[1]
    length = grad_out.shape[0]
    extra = [] if acc is None else [acc]
    inputs = 7 + len(extra) + len(ready)
    return pl.pallas_call(
        functools.partial(last_kernel, part, len(ready)),
        out_shape=[
            jax.ShapeDtypeStruct((length, total), bf16),
            jax.ShapeDtypeStruct(normed_all.shape, bf16),
        ],
        in_specs=[smem()] + [whole()] * (inputs - 1) + [anywhere()],
        out_specs=[whole(), anywhere()],
        input_output_aliases={inputs: 1},
        scratch_shapes=[VMEM((length, total), bf16), pltpu.SemaphoreType.DMA],
        compiler_params=params(24),
        cost_estimate=cost(4e9, width * total * 2),
        name="attention",
    )(index, chunk, wq, wk, wv, *extra, *ready, grad_out, tables, far(normed_all))


def back_kernel(part, n, index_ref, grads, wq, wk, wv, gain, normed_all, *rest):
    gain_in = rest[0] if part else None
    outs = rest[-(n + 4) : -4]
    gain_out, scratch, normed, sem = rest[-4:]
    rows, width = outs[0].shape
    qc, kc = wq.shape[1], wk.shape[1]
    copy = pltpu.make_async_copy(
        normed_all.at[:, pl.ds(part * width, width)], normed, sem
    )
    copy.start()
    nt = (((1,), (1,)), ((), ()))
    block = step_size(width, 768)
    for s in range(width // block):
        at = slice(part * width + s * block, part * width + (s + 1) * block)
        value = lax.dot_general(grads[:, :qc], wq[at, :], nt, preferred_element_type=f32)
        value += lax.dot_general(grads[:, qc : qc + kc], wk[at, :], nt, preferred_element_type=f32)
        value += lax.dot_general(grads[:, qc + kc :], wv[at, :], nt, preferred_element_type=f32)
        scratch[:, s * block : (s + 1) * block] = value.astype(bf16)
    for d, out in enumerate(outs):
        owner = lax.rem(index_ref[0] + d, n)
        out[...] = scratch[pl.ds(pl.multiple_of(owner * rows, rows), rows), :]
    copy.wait()
    product = scratch[...].astype(f32) * normed[...].astype(f32)
    if part:
        gain_out[:, : part * width] = gain_in[...]
    at = slice(part * width, (part + 1) * width)
    gain_out[:, at] = jnp.sum(product, axis=0, keepdims=True) / gain[:, at]


def back(index, grads, wq, wk, wv, gain, normed_all, gain_in, n, part, width):
    length, total = grads.shape
    rows = length // n
    extra = [gain_in] if part else []
    return pl.pallas_call(
        functools.partial(back_kernel, part, n),
        out_shape=[jax.ShapeDtypeStruct((rows, width), bf16)] * n
        + [jax.ShapeDtypeStruct((1, (part + 1) * width), f32)],
        in_specs=[smem()] + [whole()] * 5 + [anywhere()] + [whole()] * len(extra),
        out_specs=[whole()] * (n + 1),
        scratch_shapes=[
            VMEM((length, width), bf16),
            VMEM((length, width), bf16),
            pltpu.SemaphoreType.DMA,
        ],
        compiler_params=params(24),
        cost_estimate=cost(2 * length * width * total, width * total * 2),
        name="back_projection",
    )(index, grads, wq, wk, wv, gain, far(normed_all), *extra)


def weight_kernel(qc, kc, block, grads, normed_all, gq, gk, gv, normed, bq, bk, bv, in_sems, sems):
    steps = normed_all.shape[1] // block
    reads = []
    for s in range(steps):
        at = pl.ds(s * block, block)
        copy = pltpu.make_async_copy(normed_all.at[:, at], normed.at[:, at], in_sems.at[s])
        copy.start()
        reads.append(copy)
    tn = (((0,), (0,)), ((), ()))
    columns = (slice(0, qc), slice(qc, qc + kc), slice(qc + kc, qc + 2 * kc))
    writes = []
    for s in range(steps):
        reads[s].wait()
        x = normed[:, s * block : (s + 1) * block]
        at = pl.ds(s * block, block)
        for i, (buffer, out) in enumerate(zip((bq, bk, bv), (gq, gk, gv))):
            value = lax.dot_general(x, grads[:, columns[i]], tn, preferred_element_type=f32)
            buffer[s * block : (s + 1) * block, :] = value.astype(bf16)
            copy = pltpu.make_async_copy(buffer.at[at], out.at[at], sems.at[s * 3 + i])
            copy.start()
            writes.append(copy)
    for copy in writes:
        copy.wait()


def weights(grads, normed_all, qc, kc):
    length, total = grads.shape
    full = normed_all.shape[1]
    block = step_size(full, WEIGHT_ROWS)
    steps = full // block
    shapes = [(full, qc), (full, kc), (full, kc)]
    return pl.pallas_call(
        functools.partial(weight_kernel, qc, kc, block),
        out_shape=[jax.ShapeDtypeStruct(s, bf16) for s in shapes],
        in_specs=[whole(), anywhere()],
        out_specs=[anywhere()] * 3,
        scratch_shapes=[VMEM((length, full), bf16)]
        + [VMEM(s, bf16) for s in shapes]
        + [pltpu.SemaphoreType.DMA((steps,)), pltpu.SemaphoreType.DMA((steps * 3,))],
        compiler_params=params(24),
        cost_estimate=cost(2 * length * full * total, full * total * 2),
        name="weight_gradients",
    )(grads, far(normed_all))


def token_kernel(n, chunks, x_ref, gain_ref, *refs):
    terms, gains, (out, gain_out) = refs[: n * chunks], refs[n * chunks : -2], refs[-2:]
    gain_out[...] = sum(g[...] for g in gains)
    x = x_ref[...].astype(f32)
    inverse = lax.rsqrt(jnp.mean(x * x, axis=-1, keepdims=True) + epsilon)
    width = terms[0].shape[1]
    mean = 0.0
    for c in range(chunks):
        cols = slice(c * width, (c + 1) * width)
        summed = sum(terms[d * chunks + c][...].astype(f32) for d in range(n))
        scaled = summed * gain_ref[:, cols]
        mean += jnp.sum(scaled * (x[:, cols] * inverse), axis=-1, keepdims=True)
    mean = mean / (width * chunks)
    for c in range(chunks):
        cols = slice(c * width, (c + 1) * width)
        summed = sum(terms[d * chunks + c][...].astype(f32) for d in range(n))
        scaled = summed * gain_ref[:, cols]
        out[:, cols] = (inverse * (scaled - (x[:, cols] * inverse) * mean)).astype(bf16)


def token_gradient(x, gain, terms, gains, n, chunks):
    rows, width = x.shape
    block = rows // 4 if rows % 64 == 0 else rows
    by_rows = lambda c: pl.BlockSpec((block, c), lambda s: (s, 0))
    fixed = pl.BlockSpec((1, width), lambda s: (0, 0))
    return pl.pallas_call(
        functools.partial(token_kernel, n, chunks),
        grid=(rows // block,),
        out_shape=[jax.ShapeDtypeStruct(x.shape, bf16), jax.ShapeDtypeStruct(gain.shape, f32)],
        in_specs=[by_rows(width), fixed] + [by_rows(width // chunks)] * len(terms) + [fixed] * n,
        out_specs=[by_rows(width), fixed],
        compiler_params=params(12),
        cost_estimate=cost(1e9, x.size * 8),
        name="token_gradient",
    )(far(x), far(gain), *terms, *gains)


def grid_of(shape, n):
    rows, width = shape
    across = max(1, 8 * n // rows)
    if n % across or rows % (n // across) or width % (across * 128):
        across = 1
    return n // across, across


def cut(array, n):
    down, across = grid_of(array.shape, n)
    rows, width = array.shape
    pieces = array.reshape(down, rows // down, across, width // across)
    return pieces.transpose(0, 2, 1, 3).reshape(n, rows // down, width // across)


def mean_kernel(across, rep_ref, pieces, ours, out, mine_ref, sem):
    n, high, wide = pieces.shape
    row = pl.multiple_of(rep_ref[0] // across * high, high)
    col = pl.multiple_of(lax.rem(rep_ref[0], across) * wide, wide)
    copy = pltpu.make_async_copy(ours.at[pl.ds(row, high), pl.ds(col, wide)], mine_ref, sem)
    copy.start()
    copy.wait()
    mine = mine_ref[...]
    total = jnp.zeros_like(mine)
    for r in range(n):
        total += mine - pieces[r].astype(f32)
    total = (total / n).astype(out.dtype)
    for r in range(n):
        out[r] = total


def mean_pieces(rep, pieces, ours):
    _, across = grid_of(ours.shape, pieces.shape[0])
    return pl.pallas_call(
        functools.partial(mean_kernel, across),
        out_shape=jax.ShapeDtypeStruct(pieces.shape, bf16),
        in_specs=[smem(), whole(), anywhere()],
        out_specs=whole(),
        scratch_shapes=[VMEM(pieces.shape[1:], f32), pltpu.SemaphoreType.DMA],
        compiler_params=params(8),
        cost_estimate=cost(1e8, pieces.size * 6),
        name="mean_pieces",
    )(rep, pieces, far(ours))


def update_kernel(across, pieces, ours, momentum, new_ours, new_momentum):
    n, high, wide = pieces.shape
    for r in range(n):
        row, col = r // across * high, r % across * wide
        at = slice(row, row + high), slice(col, col + wide)
        mean_delta = pieces[r].astype(f32)
        speed = outer_momentum * momentum[at] + mean_delta
        new_momentum[at] = speed
        new_ours[at] = ours[at] - outer_rate * (mean_delta + outer_momentum * speed)


def update(pieces, ours, momentum):
    _, across = grid_of(ours.shape, pieces.shape[0])
    return pl.pallas_call(
        functools.partial(update_kernel, across),
        out_shape=[jax.ShapeDtypeStruct(ours.shape, f32)] * 2,
        in_specs=[whole()] * 3,
        out_specs=[whole()] * 2,
        compiler_params=params(8),
        cost_estimate=cost(1e8, ours.size * 20),
        name="update",
    )(pieces, ours, momentum)


def send(piece, pairs):
    return lax.ppermute(piece, "tp", pairs)


def step(
    tokens,
    norm_gain,
    w_query,
    key_weight,
    value_weight,
    attention_gradient,
    global_fragment,
    momentum,
    local_fragment,
):
    x, wq, wk, wv = tokens[0], w_query[0], key_weight[0], value_weight[0]
    grad_out = attention_gradient[0]
    n, replicas = lax.axis_size("tp"), lax.axis_size("rep")
    here = lax.axis_index("tp")
    index = here.reshape(1).astype(jnp.int32)
    rows, features = x.shape
    qc, kc = wq.shape[1], wk.shape[1]
    chunks = chunk_count(features)
    width = features // chunks
    shift = lambda d: [(j, (j + d) % n) for j in range(n)]

    own = list(norm(x, norm_gain, chunks))
    arrived = [[send(piece, shift(d)) for piece in own] for d in range(1, n)]

    tables = rope_tables(rows * n, HEAD_SIZE)
    own_rows, normed_all = project_own(index, own, wq, wk, wv, tables)
    ready = [own_rows]

    rep = lax.axis_index("rep").reshape(1).astype(jnp.int32)
    pieces = lax.all_to_all(cut(local_fragment[0], replicas), "rep", 0, 0, tiled=False)
    spread = mean_pieces(rep, pieces, global_fragment)

    for d in range(1, n):
        acc = None
        owner = lax.rem(index + (n - d), n)
        for c in range(chunks if d < n - 1 else chunks - 1):
            acc, normed_all = project_part(owner, arrived[d - 1][c], wq, wk, wv, acc, normed_all, c)
        if d < n - 1:
            turn = lax.dynamic_slice_in_dim(tables, owner[0] * rows, rows, 0)
            ready.append(finish(acc, turn, qc, kc))
    last = arrived[n - 2][chunks - 1]
    grads, normed_all = last_and_attention(
        index, last, wq, wk, wv, acc, ready, grad_out, tables, normed_all, chunks - 1
    )

    terms, gain_part = [], None
    for c in range(chunks):
        *pieces_of, gain_part = back(
            index, grads, wq, wk, wv, norm_gain, normed_all, gain_part, n, c, width
        )
        terms.append(pieces_of)
    landed = [[send(terms[c][d], shift(d)) for c in range(chunks)] for d in range(1, n)]
    own_terms = [terms[c][0] for c in range(chunks)]
    gains = [gain_part] + [send(gain_part, shift(d)) for d in range(1, n)]
    grad_wq, grad_wk, grad_wv = weights(grads, normed_all, qc, kc)

    gathered = lax.all_to_all(spread, "rep", 0, 0, tiled=False)
    new_global, new_momentum = update(gathered, global_fragment, momentum)

    grad_tokens, gain_total = token_gradient(
        x, norm_gain, own_terms + [c for group in landed for c in group], gains, n, chunks
    )
    return (
        grad_wq[None],
        grad_wk[None],
        grad_wv[None],
        gain_total,
        grad_tokens[None],
        new_global,
        new_momentum,
    )


def finish_kernel(qc, kc, acc, tables, out):
    parts = acc[:, :qc], acc[:, qc : qc + kc], acc[:, qc + kc :]
    finish_projection(parts, tables[...], out, 0)


def finish(acc, tables, qc, kc):
    return pl.pallas_call(
        functools.partial(finish_kernel, qc, kc),
        out_shape=jax.ShapeDtypeStruct(acc.shape, bf16),
        in_specs=[whole()] * 2,
        out_specs=whole(),
        compiler_params=params(8),
        cost_estimate=cost(1e8, acc.size * 6),
        name="finish_projection",
    )(acc, tables)


def solution(mesh):
    placed = (
        P("rep", "tp", None),
        P("rep", None),
        P("rep", None, "tp"),
        P("rep", None, "tp"),
        P("rep", None, "tp"),
        P("rep", None, "tp"),
        P("tp", None),
        P("tp", None),
        P("rep", "tp", None),
    )
    return jax.shard_map(
        step,
        mesh=mesh,
        in_specs=placed,
        out_specs=(
            P("rep", None, "tp"),
            P("rep", None, "tp"),
            P("rep", None, "tp"),
            P("rep", None),
            P("rep", "tp", None),
            P("tp", None),
            P("tp", None),
        ),
        check_vma=False,
    )
```

time: 148 us -> 77.2 us (0.52)
  matrix products: 41.3 us -> 0 us
  Pallas kernels: 0 us -> 36.5 us
  waiting for transfers between devices: 38.9 us -> 10.1 us
  other arithmetic: 21.3 us -> 0.01 us
  starting transfers between devices: 0.12 us -> 19.1 us
  between operations: 15.7 us -> 0.88 us
  local copies, waits for them, and re-layouts: 20.8 us -> 9.91 us
  blocking collectives: 8.76 us -> 0 us
    dot_general x13 -> x0, matrix products: 38.1 us -> none  [the longest x1 5.36 us: one_block(): jnp.einsum('grqk,qgrd->kgd', score_low, query_block, preferred_element_ty...]
    pallas_call x0 -> x10, Pallas kernels: none -> 36.5 us  [the longest x1 8.34 us: project_own(): pl.pallas_call(functools.partial(own_kernel, block, min(3, steps)), out_s...]
    psum x1 -> x0, waiting for transfers between devices: 27 us -> none  [body(): mean_delta = lax.psum(delta, 'rep') / replicas]
    dot_general x2 -> x0, local copies, waits for them, and re-layouts: 13.4 us -> none  [the longest x1 8.68 us: body(): jnp.dot(normalized, weight_q, preferred_element_type=jnp.float32)]
    all_to_all x0 -> x2, starting transfers between devices: none -> 12.4 us  [the longest x1 6.39 us: step(): lax.all_to_all(cut(local_fragment[0], replicas), 'rep', 0, 0, tiled=False)]
    all_gather x1 -> x0, waiting for transfers between devices: 11.8 us -> none  [body(): normalized = lax.all_gather(normalized_local, 'tp', axis=0, tiled=True)]
    ppermute x0 -> x5, waiting for transfers between devices: none -> 10.1 us  [send(): return lax.ppermute(piece, 'tp', pairs)]
    psum x1 -> x0, blocking collectives: 8.76 us -> none  [body(): lax.psum(jnp.sum(summed_rows * normalized_input, axis=0), 'tp')]
  transfers between devices with their start and end apart: 3 -> 7, of which waited for: 2 -> 1; matrix products, arithmetic and copies ran while one was open for 49% -> 0% of each run, Pallas kernels for 0% -> 40%
where the time goes in v1:
time: 77.2 us; the launch traced here: 76.4 us
  Pallas kernels  36.5 us (47%)
  starting transfers between devices  19.1 us (25%)
  waiting for transfers between devices  10.1 us (13%)
  local copies, waits for them, and re-layouts  9.91 us (13%)
  between operations  0.88 us (1%)
    ppermute x5, waiting for transfers between devices, send(): return lax.ppermute(piece, 'tp', pairs)  10.1 us
    unnamed x32, local copies, waits for them, and re-layouts  9.91 us
    pallas_call x1, Pallas kernels, project_own(): pl.pallas_call(functools.partial(own_kernel, block, min(3, steps)), out_s...  8.34 us
    ppermute x5, starting transfers between devices, send(): return lax.ppermute(piece, 'tp', pairs)  6.63 us
    pallas_call x1, Pallas kernels, weights(): pl.pallas_call(functools.partial(weight_kernel, qc, kc, block), out_shape...  6.41 us
    all_to_all x1, starting transfers between devices, step(): lax.all_to_all(cut(local_fragment[0], replicas), 'rep', 0, 0, tiled=False)  6.39 us
    all_to_all x1, starting transfers between devices, step(): gathered = lax.all_to_all(spread, 'rep', 0, 0, tiled=False)  6.05 us
    pallas_call x2, Pallas kernels, back(): pl.pallas_call(functools.partial(back_kernel, part, n), out_shape=[jax.Sh...  5.32 us
  transfers between devices with their start and end apart: 7, of which 1 were waited for; matrix products, arithmetic and copies ran while one was open for 0% of the time, Pallas kernels for 40%

profile of v1, /device:TPU:0, one launch (start us, length us, event | category | flops | bytes accessed | tf_op | source)
XLA Modules:
  0.0 76.4 jit_solution(15919220125447355705)
XLA Ops:
  0.6 2.4 %norm.1 = (bf16[128,1536]{1,0:T(8,128)(2,1)}, bf16[128,1536]{1,0:T(8,128)(2,1)}) custom-call(bf16[128,3072]{1,0:T(8,128)(2,1)} %bitcast.34, f32[1,3072]{1,0:T(1,128)} %gain_ref.3), custom_call_target="tpu_custom_call" | custom-call | flops 1000000000 | bytes 1572864 | tf_op jit(solution)/shard_map/norm/pallas_call | solution.py:92
  3.0 3.0 %collective-permute-start.1 = (bf16[128,1536]{1,0:T(8,128)(2,1)}, bf16[128,1536]{1,0:T(8,128)(2,1)}, u32[]{:S(2)}, u32[]{:S(2)}) collective-permute-start(bf16[128,1536]{1,0:T(8,128)(2,1)} %get-tuple-element.29.refs_0_), channel_id=1, source_target_pairs={{0,1},{1,0},{2,3},{3,2},{4,5},{5,4},{6,7},{7,6},{8,9},{9,8},{10,11... | collective-permute-start | bytes 1179656 | tf_op jit(solution)/shard_map/ppermute | solution.py:528
  6.0 0.0 collective-permute-start
  6.1 6.4 %all-to-all-start = ((bf16[16,8,1536]{2,1,0:T(8,128)(2,1)}), bf16[16,8,1536]{2,1,0:T(8,128)(2,1)S(1)}, u32[]{:S(2)}, u32[]{:S(2)}) async-start(bf16[16,8,1536]{2,1,0:T(8,128)(2,1)} %bitcast.13), calls=%async_computation | async-start | bytes 786432 | tf_op jit(solution)/shard_map/all_to_all | solution.py:561
  12.5 0.0 slice-start
  12.5 0.0 copy-start.11
  12.5 1.1 %copy-done.11 = f32[256,256]{1,0:T(8,128)S(1)} copy-done((f32[256,256]{1,0:T(8,128)S(1)}, f32[256,256]{1,0:T(8,128)}, u32[]{:S(2)}) %copy-start.11) | copy-done | bytes 262168
  13.6 8.3 %own_projection.1 = (bf16[128,2048]{1,0:T(8,128)(2,1)S(1)}, bf16[256,3072]{1,0:T(8,128)(2,1)S(1)}) custom-call(s32[1]{0:T(128)} %bitcast.index_ref, f32[256,256]{1,0:T(8,128)S(1)} %copy-done.11, bf16[128,1536]{1,0:T(8,128)(2,1)} %get-tuple-element.29.refs_0_, bf16[128,1536]{1,0:T(8,128)(2,1)} %get-tuple-element.28.refs_1_, bf16[3072,1024]{1,0:T(8,128)(2,1)} %bitcast.16, ...), custom_call_target="tpu_custom_call" | custom-call | flops 5000000000 | bytes 12582912 | tf_op jit(solution)/shard_map/own_projection/pallas_call | solution.py:177
  21.9 0.0 copy-start.4
  21.9 1.2 %copy-done.4 = bf16[256,3072]{1,0:T(8,128)(2,1)} copy-done((bf16[256,3072]{1,0:T(8,128)(2,1)}, bf16[256,3072]{1,0:T(8,128)(2,1)S(1)}, u32[]{:S(2)}) %copy-start.4) | copy-done | bytes 1572888
  23.1 0.0 collective-permute-done.1.chunk
  23.1 0.0 slice-done
  23.1 0.0 copy-done.1
  23.1 0.0 copy-done.2
  23.2 0.0 copy-start.10
  23.2 0.0 copy-start.12
  23.2 2.1 %part_projection.1 = (f32[128,2048]{1,0:T(8,128)S(1)}, bf16[256,3072]{1,0:T(8,128)(2,1)}) custom-call(s32[1]{0:T(128)S(6)} %rem.18.row_ref, bf16[128,1536]{1,0:T(8,128)(2,1)} %collective-permute-done.1.chunk, bf16[3072,1024]{1,0:T(8,128)(2,1)S(1)} %bitcast.19, bf16[3072,512]{1,0:T(8,128)(2,1)S(1)} %bitcast.24, ...), custom_call_target="tpu_custom_call", output_to_operand_aliasing={{1}: (5, {})} | custom-call | flops 805306368 | bytes 6291456 | tf_op jit(solution)/shard_map/part_projection/pallas_call | solution.py:217
  25.3 0.0 collective-permute-done.chunk
  25.3 0.0 copy-done.10
  25.3 0.0 copy-done.12
  25.3 0.0 copy-start.13
  25.3 5.0 %attention.1 = (bf16[256,2048]{1,0:T(8,128)(2,1)S(1)}, bf16[256,3072]{1,0:T(8,128)(2,1)}) custom-call(s32[1]{0:T(128)} %bitcast.index_ref, bf16[128,1536]{1,0:T(8,128)(2,1)} %collective-permute-done.chunk, bf16[3072,1024]{1,0:T(8,128)(2,1)S(1)} %bitcast.20, bf16[3072,512]{1,0:T(8,128)(2,1)S(1)} %bitcast.25, ...), custom_call_target="tpu_custom_call", output_to_operand_aliasing={{1}: (9, {})} | custom-call | flops 4000000000 | bytes 6291456 | tf_op jit(solution)/shard_map/attention/pallas_call | solution.py:310
  30.3 0.0 copy-start.5
  30.3 1.0 %copy-done.5 = bf16[256,2048]{1,0:T(8,128)(2,1)} copy-done((bf16[256,2048]{1,0:T(8,128)(2,1)}, bf16[256,2048]{1,0:T(8,128)(2,1)S(1)}, u32[]{:S(2)}) %copy-start.5) | copy-done | bytes 1048600
  31.2 0.0 all-to-all-done.pieces
  31.2 0.9 %mean_pieces.1 = bf16[16,8,1536]{2,1,0:T(8,128)(2,1)S(1)} custom-call(s32[1]{0:T(128)} %bitcast.10.rep_ref, bf16[16,8,1536]{2,1,0:T(8,128)(2,1)S(1)} %all-to-all-done.pieces, f32[64,3072]{1,0:T(8,128)} %ours.3), custom_call_target="tpu_custom_call" | custom-call | flops 100000000 | bytes 1179648 | tf_op jit(solution)/shard_map/mean_pieces/pallas_call | solution.py:491
  32.1 0.0 copy-start.8
  32.2 0.7 copy-done.8
  32.9 6.0 %all-to-all-start.1 = ((bf16[16,8,1536]{2,1,0:T(8,128)(2,1)}), bf16[16,8,1536]{2,1,0:T(8,128)(2,1)}, u32[]{:S(2)}, u32[]{:S(2)}) async-start(bf16[16,8,1536]{2,1,0:T(8,128)(2,1)} %copy-done.8), calls=%async_computation.1 | async-start | bytes 786432 | tf_op jit(solution)/shard_map/all_to_all | solution.py:588
  39.0 0.0 copy-start
  39.0 2.8 %copy-done = bf16[1,3072,1024]{2,1,0:T(8,128)(2,1)S(1)} copy-done((bf16[1,3072,1024]{2,1,0:T(8,128)(2,1)S(1)}, bf16[1,3072,1024]{2,1,0:T(8,128)(2,1)}, u32[]{:S(2)}) %copy-start) | copy-done | bytes 6291480
  41.8 1.9 %copy-done.3 = bf16[1,3072,512]{2,1,0:T(8,128)(2,1)S(1)} copy-done((bf16[1,3072,512]{2,1,0:T(8,128)(2,1)S(1)}, bf16[1,3072,512]{2,1,0:T(8,128)(2,1)}, u32[]{:S(2)}) %copy-start.3) | copy-done | bytes 3145752
  43.6 1.2 %copy-done.6 = bf16[256,2048]{1,0:T(8,128)(2,1)S(1)} copy-done((bf16[256,2048]{1,0:T(8,128)(2,1)S(1)}, bf16[256,2048]{1,0:T(8,128)(2,1)}, u32[]{:S(2)}) %copy-start.6) | copy-done | bytes 1048600
  44.9 2.7 %back_projection.2 = (bf16[128,1536]{1,0:T(8,128)(2,1)S(1)}, bf16[128,1536]{1,0:T(8,128)(2,1)S(1)}, f32[1,1536]{1,0:T(1,128)S(1)}) custom-call(s32[1]{0:T(128)} %bitcast.index_ref, bf16[256,2048]{1,0:T(8,128)(2,1)S(1)} %copy-done.6, bf16[3072,1024]{1,0:T(8,128)(2,1)S(1)} %bitcast.21, bf16[3072,512]{1,0:T(8,128)(2,1)S(1)} %bitcast.26, ...), custom_call_target="tpu_custom_call" | custom-call | flops 1610612736 | bytes 6291456 | tf_op jit(solution)/shard_map/back_projection/pallas_call | solution.py:359
  47.5 2.7 %back_projection.3 = (bf16[128,1536]{1,0:T(8,128)(2,1)S(1)}, bf16[128,1536]{1,0:T(8,128)(2,1)S(1)}, f32[1,3072]{1,0:T(1,128)S(1)}) custom-call(s32[1]{0:T(128)} %bitcast.index_ref, bf16[256,2048]{1,0:T(8,128)(2,1)S(1)} %copy-done.6, bf16[3072,1024]{1,0:T(8,128)(2,1)S(1)} %bitcast.22, bf16[3072,512]{1,0:T(8,128)(2,1)S(1)} %bitcast.27, ...), custom_call_target="tpu_custom_call" | custom-call | flops 1610612736 | bytes 6291456 | tf_op jit(solution)/shard_map/back_projection/pallas_call | solution.py:359
  50.2 1.6 %collective-permute-start.3 = (bf16[128,1536]{1,0:T(8,128)(2,1)S(1)}, bf16[128,1536]{1,0:T(8,128)(2,1)S(1)}, u32[]{:S(2)}, u32[]{:S(2)}) collective-permute-start(bf16[128,1536]{1,0:T(8,128)(2,1)S(1)} %get-tuple-element.43), channel_id=1, source_target_pairs={{0,1},{1,0},{2,3},{3,2},{4,5},{5,4},{6,7},{7,6},{8,9},{9,8},{10,11... | collective-permute-start | bytes 1179656 | tf_op jit(solution)/shard_map/ppermute | solution.py:528
  51.8 0.5 collective-permute-start.2
  52.3 1.5 %collective-permute-start.4 = (f32[1,3072]{1,0:T(1,128)S(1)}, f32[1,3072]{1,0:T(1,128)S(1)}, u32[]{:S(2)}, u32[]{:S(2)}) collective-permute-start(f32[1,3072]{1,0:T(1,128)S(1)} %get-tuple-element.44.refs_4_), channel_id=1, source_target_pairs={{0,1},{1,0},{2,3},{3,2},{4,5},{5,4},{6,7},{7,6},{8,9},{9,8},{10,11... | collective-permute-start | bytes 36872 | tf_op jit(solution)/shard_map/ppermute | solution.py:528
  53.8 6.4 %weight_gradients.1 = (bf16[3072,1024]{1,0:T(8,128)(2,1)}, bf16[3072,512]{1,0:T(8,128)(2,1)}, bf16[3072,512]{1,0:T(8,128)(2,1)}) custom-call(bf16[256,2048]{1,0:T(8,128)(2,1)S(1)} %copy-done.6, bf16[256,3072]{1,0:T(8,128)(2,1)} %get-tuple-element.35.normed_all), custom_call_target="tpu_custom_call" | custom-call | flops 3221225472 | bytes 12582912 | tf_op jit(solution)/shard_map/weight_gradients/pallas_call | solution.py:407
  60.2 0.0 copy-start.7
  60.2 0.0 copy-start.9
  60.3 10.1 %collective-permute-done.4.refs_5_ = f32[1,3072]{1,0:T(1,128)S(1)} collective-permute-done((f32[1,3072]{1,0:T(1,128)S(1)}, f32[1,3072]{1,0:T(1,128)S(1)}, u32[]{:S(2)}, u32[]{:S(2)}) %collective-permute-start.4) | collective-permute-done | bytes 12320 | tf_op jit(solution)/shard_map/ppermute | solution.py:528
  70.3 0.0 collective-permute-done.3.refs_3_
  70.3 0.0 collective-permute-done.2.refs_2_
  70.3 3.8 %token_gradient.1 = (bf16[128,3072]{1,0:T(8,128)(2,1)}, f32[1,3072]{1,0:T(1,128)}) custom-call(bf16[128,3072]{1,0:T(8,128)(2,1)} %bitcast.35, f32[1,3072]{1,0:T(1,128)} %gain_ref.3, bf16[128,1536]{1,0:T(8,128)(2,1)S(1)} %get-tuple-element.39.refs_0_, bf16[128,1536]{1,0:T(8,128)(2,1)S(1)} %get-tuple-element.41.refs_1_, ...), custom_call_target="tpu_custom_call" | custom-call | flops 1000000000 | bytes 3145728 | tf_op jit(solution)/shard_map/token_gradient/pallas_call | solution.py:446
  74.1 0.0 all-to-all-done.1.pieces
  74.1 0.0 copy-done.7
  74.1 2.3 %update.1 = (f32[64,3072]{1,0:T(8,128)}, f32[64,3072]{1,0:T(8,128)}) custom-call(bf16[16,8,1536]{2,1,0:T(8,128)(2,1)} %all-to-all-done.1.pieces, f32[64,3072]{1,0:T(8,128)S(1)} %copy-done.7, f32[64,3072]{1,0:T(8,128)S(1)} %copy-done.9), custom_call_target="tpu_custom_call" | custom-call | flops 100000000 | bytes 3932160 | tf_op jit(solution)/shard_map/update/pallas_call | solution.py:516
  (9 shorter events, 0.0 us)
Async XLA Ops:
  3.0 20.1 %collective-permute-start.1 = (bf16[128,1536]{1,0:T(8,128)(2,1)}, bf16[128,1536]{1,0:T(8,128)(2,1)}, u32[]{:S(2)}, u32[]{:S(2)}) collective-permute-start(bf16[128,1536]{1,0:T(8,128)(2,1)} %get-tuple-element.29.refs_0_), channel_id=1, source_target_pairs={{0,1},{1,0},{2,3},{3,2},{4,5},{5,4},{6,7},{7,6},{8,9},{9,8},{10,11... | collective-permute-start | bytes 1179656 | tf_op jit(solution)/shard_map/ppermute | solution.py:528
  6.0 19.2 %collective-permute-start = (bf16[128,1536]{1,0:T(8,128)(2,1)}, bf16[128,1536]{1,0:T(8,128)(2,1)}, u32[]{:S(2)}, u32[]{:S(2)}) collective-permute-start(bf16[128,1536]{1,0:T(8,128)(2,1)} %get-tuple-element.28.refs_1_), channel_id=1, source_target_pairs={{0,1},{1,0},{2,3},{3,2},{4,5},{5,4},{6,7},{7,6},{8,9},{9,8},{10,11... | collective-permute-start | bytes 1179656 | tf_op jit(solution)/shard_map/ppermute | solution.py:528
  6.1 25.2 %all-to-all-start = ((bf16[16,8,1536]{2,1,0:T(8,128)(2,1)}), bf16[16,8,1536]{2,1,0:T(8,128)(2,1)S(1)}, u32[]{:S(2)}, u32[]{:S(2)}) async-start(bf16[16,8,1536]{2,1,0:T(8,128)(2,1)} %bitcast.13), calls=%async_computation | async-start | bytes 786432 | tf_op jit(solution)/shard_map/all_to_all | solution.py:561
  12.5 10.7 %slice-start = ((s8[6291456]{0:T(1024)(128)(4,1)}), s8[4194304]{0:T(1024)(128)(4,1)S(1)}, s32[]{:S(2)}) async-start(s8[6291456]{0:T(1024)(128)(4,1)} %bitcast.17), calls=%async_computation.2 | async-start | bytes 8388608
  12.5 1.1 %copy-start.11 = (f32[256,256]{1,0:T(8,128)S(1)}, f32[256,256]{1,0:T(8,128)}, u32[]{:S(2)}) copy-start(f32[256,256]{1,0:T(8,128)} %constant.18.clone.tables.rest_3_) | copy-start | bytes 786436
  13.6 9.5 %slice-start.1 = ((s8[6291456]{0:T(1024)(128)(4,1)}), s8[2097152]{0:T(1024)(128)(4,1)S(1)}, s32[]{:S(2)}) async-start(s8[6291456]{0:T(1024)(128)(4,1)} %bitcast.17), calls=%async_computation.3 | async-start | bytes 4194304
  13.6 9.5 %copy-start.1 = (bf16[1,3072,512]{2,1,0:T(8,128)(2,1)S(1)}, bf16[1,3072,512]{2,1,0:T(8,128)(2,1)}, u32[]{:S(2)}) copy-start(bf16[1,3072,512]{2,1,0:T(8,128)(2,1)} %param.13) | copy-start | bytes 9437188
  13.6 9.5 %copy-start.2 = (bf16[1,3072,512]{2,1,0:T(8,128)(2,1)S(1)}, bf16[1,3072,512]{2,1,0:T(8,128)(2,1)}, u32[]{:S(2)}) copy-start(bf16[1,3072,512]{2,1,0:T(8,128)(2,1)} %param.14) | copy-start | bytes 9437188
  21.9 1.2 %copy-start.4 = (bf16[256,3072]{1,0:T(8,128)(2,1)}, bf16[256,3072]{1,0:T(8,128)(2,1)S(1)}, u32[]{:S(2)}) copy-start(bf16[256,3072]{1,0:T(8,128)(2,1)S(1)} %get-tuple-element.30.rest_0_) | copy-start | bytes 4718596
  23.2 2.1 %copy-start.10 = (bf16[1,256,1024]{2,1,0:T(8,128)(2,1)S(1)}, bf16[1,256,1024]{2,1,0:T(8,128)(2,1)}, u32[]{:S(2)}) copy-start(bf16[1,256,1024]{2,1,0:T(8,128)(2,1)} %param.15) | copy-start | bytes 1572868
  23.2 2.1 %copy-start.12 = (f32[256,256]{1,0:T(8,128)S(1)}, f32[256,256]{1,0:T(8,128)}, u32[]{:S(2)}) copy-start(f32[256,256]{1,0:T(8,128)} %constant.18.clone.tables.rest_3_) | copy-start | bytes 786436
  25.3 13.7 %copy-start.13 = (f32[1,3072]{1,0:T(1,128)S(1)}, f32[1,3072]{1,0:T(1,128)}, u32[]{:S(2)}) copy-start(f32[1,3072]{1,0:T(1,128)} %gain_ref.3) | copy-start | bytes 36868
  30.3 1.0 %copy-start.5 = (bf16[256,2048]{1,0:T(8,128)(2,1)}, bf16[256,2048]{1,0:T(8,128)(2,1)S(1)}, u32[]{:S(2)}) copy-start(bf16[256,2048]{1,0:T(8,128)(2,1)S(1)} %get-tuple-element.34.grads) | copy-start | bytes 3145732
  32.1 0.7 copy-start.8
  32.9 41.2 %all-to-all-start.1 = ((bf16[16,8,1536]{2,1,0:T(8,128)(2,1)}), bf16[16,8,1536]{2,1,0:T(8,128)(2,1)}, u32[]{:S(2)}, u32[]{:S(2)}) async-start(bf16[16,8,1536]{2,1,0:T(8,128)(2,1)} %copy-done.8), calls=%async_computation.1 | async-start | bytes 786432 | tf_op jit(solution)/shard_map/all_to_all | solution.py:588
  39.0 2.8 %copy-start = (bf16[1,3072,1024]{2,1,0:T(8,128)(2,1)S(1)}, bf16[1,3072,1024]{2,1,0:T(8,128)(2,1)}, u32[]{:S(2)}) copy-start(bf16[1,3072,1024]{2,1,0:T(8,128)(2,1)} %param.12) | copy-start | bytes 18874372
  41.7 1.9 %copy-start.3 = (bf16[1,3072,512]{2,1,0:T(8,128)(2,1)S(1)}, bf16[1,3072,512]{2,1,0:T(8,128)(2,1)}, u32[]{:S(2)}) copy-start(bf16[1,3072,512]{2,1,0:T(8,128)(2,1)} %param.14) | copy-start | bytes 9437188
  43.6 1.2 %copy-start.6 = (bf16[256,2048]{1,0:T(8,128)(2,1)S(1)}, bf16[256,2048]{1,0:T(8,128)(2,1)}, u32[]{:S(2)}) copy-start(bf16[256,2048]{1,0:T(8,128)(2,1)} %copy-done.5) | copy-start | bytes 3145732
  50.2 20.1 %collective-permute-start.3 = (bf16[128,1536]{1,0:T(8,128)(2,1)S(1)}, bf16[128,1536]{1,0:T(8,128)(2,1)S(1)}, u32[]{:S(2)}, u32[]{:S(2)}) collective-permute-start(bf16[128,1536]{1,0:T(8,128)(2,1)S(1)} %get-tuple-element.43), channel_id=1, source_target_pairs={{0,1},{1,0},{2,3},{3,2},{4,5},{5,4},{6,7},{7,6},{8,9},{9,8},{10,11... | collective-permute-start | bytes 1179656 | tf_op jit(solution)/shard_map/ppermute | solution.py:528
  51.8 18.5 %collective-permute-start.2 = (bf16[128,1536]{1,0:T(8,128)(2,1)S(1)}, bf16[128,1536]{1,0:T(8,128)(2,1)S(1)}, u32[]{:S(2)}, u32[]{:S(2)}) collective-permute-start(bf16[128,1536]{1,0:T(8,128)(2,1)S(1)} %get-tuple-element.42), channel_id=1, source_target_pairs={{0,1},{1,0},{2,3},{3,2},{4,5},{5,4},{6,7},{7,6},{8,9},{9,8},{10,11... | collective-permute-start | bytes 1179656 | tf_op jit(solution)/shard_map/ppermute | solution.py:528
  52.3 18.0 %collective-permute-start.4 = (f32[1,3072]{1,0:T(1,128)S(1)}, f32[1,3072]{1,0:T(1,128)S(1)}, u32[]{:S(2)}, u32[]{:S(2)}) collective-permute-start(f32[1,3072]{1,0:T(1,128)S(1)} %get-tuple-element.44.refs_4_), channel_id=1, source_target_pairs={{0,1},{1,0},{2,3},{3,2},{4,5},{5,4},{6,7},{7,6},{8,9},{9,8},{10,11... | collective-permute-start | bytes 36872 | tf_op jit(solution)/shard_map/ppermute | solution.py:528
  60.2 13.9 %copy-start.7 = (f32[64,3072]{1,0:T(8,128)S(1)}, f32[64,3072]{1,0:T(8,128)}, u32[]{:S(2)}) copy-start(f32[64,3072]{1,0:T(8,128)} %ours.3) | copy-start | bytes 2359300
  60.2 13.9 %copy-start.9 = (f32[64,3072]{1,0:T(8,128)S(1)}, f32[64,3072]{1,0:T(8,128)}, u32[]{:S(2)}) copy-start(f32[64,3072]{1,0:T(8,128)} %momentum.1) | copy-start | bytes 2359300

commit v2 on v1

v2 whole, which is shorter than its diff:
```python
import functools
import math

import jax
import jax.numpy as jnp
import numpy as np
from jax import lax
from jax.experimental import pallas as pl
from jax.experimental.pallas import tpu as pltpu
from jax.sharding import PartitionSpec as P


HEAD_SIZE = 128

epsilon = 1e-05
rope_base = 500000.0
outer_rate = 0.7
outer_momentum = 0.9

VMEM = pltpu.VMEM
f32, bf16 = jnp.float32, jnp.bfloat16

WEIGHT_ROWS = 768
TOKEN_STEPS = 2


def whole():
    return pl.BlockSpec(memory_space=VMEM)


def anywhere():
    return pl.BlockSpec(memory_space=pl.ANY)


def far(array):
    return pltpu.with_memory_space_constraint(array, pltpu.HBM)


def smem():
    return pl.BlockSpec(memory_space=pltpu.SMEM)


def params(mib):
    return pltpu.CompilerParams(vmem_limit_bytes=mib << 20)


def cost(flops, nbytes):
    return pl.CostEstimate(flops=int(flops), bytes_accessed=int(nbytes), transcendentals=0)


def rope_tables(length, width):
    middle = width // 2
    frequency = rope_base ** (-2.0 * np.arange(middle) / width)
    angles = np.arange(length)[:, None] * frequency[None, :]
    cosine, sine = np.cos(angles), np.sin(angles)
    tables = (cosine, cosine, -sine, sine)
    return jnp.asarray(np.concatenate(tables, 1).astype(np.float32))


def rope(v, cosine, sine):
    return v * cosine + pltpu.roll(v, v.shape[-1] // 2, 1) * sine


def unrope(v, cosine, sine):
    return v * cosine - pltpu.roll(v, v.shape[-1] // 2, 1) * sine


def chunk_widths(width, thirds):
    first = width * thirds // 3 // 128 * 128
    return (first, width - first) if first else (width,)


def step_size(width, most):
    for n in range(most, 0, -128):
        if width % n == 0:
            return n
    return width


def norm_kernel(x_ref, gain_ref, *outs):
    x = x_ref[...].astype(f32)
    inverse = lax.rsqrt(jnp.mean(x * x, axis=-1, keepdims=True) + epsilon)
    normed = ((x * inverse) * gain_ref[...]).astype(bf16)
    at = 0
    for out in outs:
        out[...] = normed[:, at : at + out.shape[1]]
        at += out.shape[1]


def norm(x, gain, widths):
    rows = x.shape[0]
    return pl.pallas_call(
        norm_kernel,
        out_shape=[jax.ShapeDtypeStruct((rows, w), bf16) for w in widths],
        in_specs=[whole()] * 2,
        out_specs=[whole()] * len(widths),
        compiler_params=params(8),
        cost_estimate=cost(1.0e9, x.size * 4),
        name="norm",
    )(far(x), far(gain))


def project(chunk, wq, wk, wv, rows):
    return [jnp.dot(chunk, w[rows, :], preferred_element_type=f32) for w in (wq, wk, wv)]


def finish_projection(parts, tables, out, row):
    rows = tables.shape[0]
    cosine, sine = tables[:, :HEAD_SIZE], tables[:, HEAD_SIZE:]
    at = 0
    for part, turned in zip(parts, (True, True, False)):
        for h in range(part.shape[1] // HEAD_SIZE):
            piece = part[:, h * HEAD_SIZE : (h + 1) * HEAD_SIZE]
            if turned:
                piece = rope(piece, cosine, sine)
            out[pl.ds(row, rows), at : at + HEAD_SIZE] = piece.astype(bf16)
            at += HEAD_SIZE


def keep(chunk, normed_all, row, at, sem):
    rows, width = chunk.shape
    place = normed_all.at[pl.ds(row, rows), pl.ds(at, width)]
    copy = pltpu.make_async_copy(chunk, place, sem)
    copy.start()
    return copy


def own_kernel(block, depth, index_ref, tables, *refs):
    chunks = refs[:-11]
    wq, wk, wv, out, normed_all, bq, bk, bv, acc, sems, keep_sems = refs[-11:]
    rows = chunks[0].shape[0]
    start = pl.multiple_of(index_ref[0] * rows, rows)
    steps = wq.shape[0] // block
    per_chunk = [ref.shape[1] // block for ref in chunks]
    blocks = [
        (ref, at * block) for ref, count in zip(chunks, per_chunk) for at in range(count)
    ]
    sources, buffers = (wq, wk, wv), (bq, bk, bv)

    def fetch(s):
        part = pl.ds(s * block, block)
        copies = [
            pltpu.make_async_copy(sources[i].at[part], buffers[i].at[part], sems.at[s * 3 + i])
            for i in range(3)
        ]
        for copy in copies:
            copy.start()
        return copies

    flights = [fetch(s) for s in range(depth)]
    kept = [
        keep(ref, normed_all, start, sum(per_chunk[:c]) * block, keep_sems.at[c])
        for c, ref in enumerate(chunks)
    ]
    for s in range(steps):
        for copy in flights[s]:
            copy.wait()
        if s + depth < steps:
            flights.append(fetch(s + depth))
        ref, at = blocks[s]
        parts = project(ref[:, at : at + block], bq, bk, bv, slice(s * block, (s + 1) * block))
        at = 0
        for part in parts:
            cols = slice(at, at + part.shape[1])
            if s == 0:
                acc[:, cols] = part
            else:
                acc[:, cols] += part
            at += part.shape[1]
    qc, kc = wq.shape[1], wk.shape[1]
    parts = acc[:, :qc], acc[:, qc : qc + kc], acc[:, qc + kc :]
    finish_projection(parts, tables[pl.ds(start, rows), :], out, 0)
    for copy in kept:
        copy.wait()


def project_own(index, chunks, wq, wk, wv, tables):
    rows = chunks[0].shape[0]
    qc, kc = wq.shape[1], wk.shape[1]
    block = step_size(math.gcd(*[c.shape[1] for c in chunks]), 512)
    full = wq.shape[0]
    steps = full // block
    total = qc + 2 * kc
    return pl.pallas_call(
        functools.partial(own_kernel, block, min(3, steps)),
        out_shape=[
            jax.ShapeDtypeStruct((rows, total), bf16),
            jax.ShapeDtypeStruct((tables.shape[0], full), bf16),
        ],
        in_specs=[smem(), whole()] + [whole()] * len(chunks) + [anywhere()] * 3,
        out_specs=[whole(), anywhere()],
        scratch_shapes=[
            VMEM((full, qc), bf16),
            VMEM((full, kc), bf16),
            VMEM((full, kc), bf16),
            VMEM((rows, total), f32),
            pltpu.SemaphoreType.DMA((steps * 3,)),
            pltpu.SemaphoreType.DMA((len(chunks),)),
        ],
        compiler_params=params(20),
        cost_estimate=cost(5e9, full * total * 2),
        name="own_projection",
    )(index, tables, *chunks, *[far(w) for w in (wq, wk, wv)])


def part_kernel(offset, row_ref, chunk, wq, wk, wv, *rest):
    out, normed_all, sem = rest[-3:]
    acc_in = rest[0] if len(rest) > 4 else None
    rows, width = chunk.shape
    kept = keep(chunk, normed_all, pl.multiple_of(row_ref[0] * rows, rows), offset, sem)
    at = 0
    for value in project(chunk[...], wq, wk, wv, slice(offset, offset + width)):
        cols = slice(at, at + value.shape[1])
        out[:, cols] = value if acc_in is None else acc_in[:, cols] + value
        at += value.shape[1]
    kept.wait()


def project_part(owner, chunk, wq, wk, wv, acc, normed_all, offset):
    rows, width = chunk.shape
    total = wq.shape[1] + 2 * wk.shape[1]
    extra = [] if acc is None else [acc]
    inputs = 5 + len(extra)
    return pl.pallas_call(
        functools.partial(part_kernel, offset),
        out_shape=[
            jax.ShapeDtypeStruct((rows, total), f32),
            jax.ShapeDtypeStruct(normed_all.shape, bf16),
        ],
        in_specs=[smem()] + [whole()] * (4 + len(extra)) + [anywhere()],
        out_specs=[whole(), anywhere()],
        input_output_aliases={inputs: 1},
        scratch_shapes=[pltpu.SemaphoreType.DMA],
        compiler_params=params(20),
        cost_estimate=cost(2 * rows * width * total, width * total * 2),
        name="part_projection",
    )(owner, chunk, wq, wk, wv, *extra, far(normed_all))


def attention(all_rows, grad_out, tables, out, qc, kc, block):
    length = all_rows.shape[0]
    group = qc // kc
    scale = HEAD_SIZE ** (-0.5)
    nt = (((1,), (1,)), ((), ()))
    tn = (((0,), (0,)), ((), ()))
    key = lax.broadcasted_iota(jnp.int32, (block, block), 0)
    query = lax.broadcasted_iota(jnp.int32, (block, block), 1)
    allowed = jnp.concatenate([key <= query] * group, 1)
    blocks = length // block
    dk, dv = {}, {}

    def head(g, r):
        return slice((g * group + r) * HEAD_SIZE, (g * group + r + 1) * HEAD_SIZE)

    def kcols(g):
        return slice(qc + g * HEAD_SIZE, qc + (g + 1) * HEAD_SIZE)

    def vcols(g):
        return slice(qc + kc + g * HEAD_SIZE, qc + kc + (g + 1) * HEAD_SIZE)

    def opening(g, a):
        rows, keys = slice(a * block, (a + 1) * block), (a + 1) * block
        q = jnp.concatenate([all_rows[rows, head(g, r)] for r in range(group)], 0)
        do = jnp.concatenate([grad_out[rows, head(g, r)] for r in range(group)], 0)
        s = lax.dot_general(all_rows[:keys, kcols(g)], q, nt, preferred_element_type=f32)
        gprob = lax.dot_general(all_rows[:keys, vcols(g)], do, nt, preferred_element_type=f32)
        return g, a, q, do, s, gprob

    def closing(g, a, q, do, s, gprob):
        rows, keys = slice(a * block, (a + 1) * block), (a + 1) * block
        s = s * scale
        corner = jnp.where(allowed, s[keys - block :], -jnp.inf)
        s = corner if a == 0 else jnp.concatenate([s[: keys - block], corner], 0)
        powers = jnp.exp(s - jnp.max(s, axis=0, keepdims=True))
        prob = powers * (1.0 / jnp.sum(powers, axis=0, keepdims=True))
        inner = jnp.sum(gprob * prob, axis=0, keepdims=True)
        low = prob.astype(bf16)
        ds = (prob * (gprob - inner) * scale).astype(bf16)
        part_v = jnp.dot(low, do, preferred_element_type=f32)
        part_k = jnp.dot(ds, q, preferred_element_type=f32)
        dq = lax.dot_general(all_rows[:keys, kcols(g)], ds, tn, preferred_element_type=f32).T
        for b in range(a + 1):
            piece = slice(b * block, (b + 1) * block)
            dv[b] = dv[b] + part_v[piece] if b < a else part_v[piece]
            dk[b] = dk[b] + part_k[piece] if b < a else part_k[piece]
        cosine, sine = tables[rows, :HEAD_SIZE], tables[rows, HEAD_SIZE:]
        for r in range(group):
            piece = unrope(dq[r * block : (r + 1) * block], cosine, sine)
            out[rows, head(g, r)] = piece.astype(bf16)
        if a < blocks - 1:
            return
        for b in range(blocks):
            rows = slice(b * block, (b + 1) * block)
            cosine, sine = tables[rows, :HEAD_SIZE], tables[rows, HEAD_SIZE:]
            out[rows, kcols(g)] = unrope(dk[b], cosine, sine).astype(bf16)
            out[rows, vcols(g)] = dv[b].astype(bf16)

    units = [(g, a) for g in range(kc // HEAD_SIZE) for a in range(blocks)]
    waiting = [opening(*unit) for unit in units[:2]]
    for i in range(len(units)):
        if i + 2 < len(units):
            waiting.append(opening(*units[i + 2]))
        closing(*waiting.pop(0))


def last_kernel(offset, others, index_ref, chunk, wq, wk, wv, *rest):
    extra = len(rest) - (2 * others + 9)
    acc_in = rest[0] if extra else None
    ready = rest[extra : extra + others]
    grad_out, tables, _, out, normed_all, *outs, all_rows, scratch, sem = rest[-(others + 9) :]
    rows, width = chunk.shape
    qc, kc = wq.shape[1], wk.shape[1]
    n = others + 1
    start = pl.multiple_of(lax.rem(index_ref[0] + 1, n) * rows, rows)
    kept = keep(chunk, normed_all, start, offset, sem)
    for d, ref in enumerate(ready):
        owner = lax.rem(index_ref[0] + (n - d), n)
        all_rows[pl.ds(pl.multiple_of(owner * rows, rows), rows), :] = ref[...]
    parts = project(chunk[...], wq, wk, wv, slice(offset, offset + width))
    if acc_in is not None:
        before = acc_in[:, :qc], acc_in[:, qc : qc + kc], acc_in[:, qc + kc :]
        parts = [b + p for b, p in zip(before, parts)]
    finish_projection(parts, tables[pl.ds(start, rows), :], all_rows, start)
    attention(all_rows, grad_out, tables, out, qc, kc, rows)
    spread_back(0, n, index_ref[0], out, wq, wk, wv, outs, scratch)
    kept.wait()


def last_and_attention(index, chunk, wq, wk, wv, acc, ready, grad_out, tables, normed_all, offset, first):
    rows, width = chunk.shape
    total = wq.shape[1] + 2 * wk.shape[1]
    length = grad_out.shape[0]
    extra = [] if acc is None else [acc]
    inputs = 7 + len(extra) + len(ready)
    return pl.pallas_call(
        functools.partial(last_kernel, offset, len(ready)),
        out_shape=[
            jax.ShapeDtypeStruct((length, total), bf16),
            jax.ShapeDtypeStruct(normed_all.shape, bf16),
        ]
        + [jax.ShapeDtypeStruct((rows, first), bf16)] * (len(ready) + 1),
        in_specs=[smem()] + [whole()] * (inputs - 1) + [anywhere()],
        out_specs=[whole(), anywhere()] + [whole()] * (len(ready) + 1),
        input_output_aliases={inputs: 1},
        scratch_shapes=[
            VMEM((length, total), bf16),
            VMEM((length, first), bf16),
            pltpu.SemaphoreType.DMA,
        ],
        compiler_params=params(24),
        cost_estimate=cost(4e9, width * total * 2),
        name="attention",
    )(index, chunk, wq, wk, wv, *extra, *ready, grad_out, tables, far(normed_all))


def spread_back(offset, n, index, grads, wq, wk, wv, outs, scratch):
    rows, width = outs[0].shape
    qc, kc = wq.shape[1], wk.shape[1]
    nt = (((1,), (1,)), ((), ()))
    block = step_size(width, 1024)
    for s in range(width // block):
        at = slice(offset + s * block, offset + (s + 1) * block)
        value = lax.dot_general(grads[:, :qc], wq[at, :], nt, preferred_element_type=f32)
        value += lax.dot_general(grads[:, qc : qc + kc], wk[at, :], nt, preferred_element_type=f32)
        value += lax.dot_general(grads[:, qc + kc :], wv[at, :], nt, preferred_element_type=f32)
        scratch[:, s * block : (s + 1) * block] = value.astype(bf16)
    for d, out in enumerate(outs):
        place = pl.multiple_of(lax.rem(index + d, n) * rows, rows)
        out[...] = scratch[pl.ds(place, rows), :]


def back_kernel(offset, n, index_ref, grads, wq, wk, wv, *rest):
    spread_back(offset, n, index_ref[0], grads, wq, wk, wv, rest[:-1], rest[-1])


def back(index, grads, wq, wk, wv, n, offset, width):
    length, total = grads.shape
    rows = length // n
    return pl.pallas_call(
        functools.partial(back_kernel, offset, n),
        out_shape=[jax.ShapeDtypeStruct((rows, width), bf16)] * n,
        in_specs=[smem()] + [whole()] * 4,
        out_specs=[whole()] * n,
        scratch_shapes=[VMEM((length, width), bf16)],
        compiler_params=params(24),
        cost_estimate=cost(2 * length * width * total, width * total * 2),
        name="back_projection",
    )(index, grads, wq, wk, wv)


def weight_kernel(qc, kc, block, n, widths, index_ref, grads, gain, normed_all, *refs):
    chunks = len(widths)
    terms = refs[: n * chunks]
    gq, gk, gv, gg, normed, turned, bq, bk, bv, in_sems, term_sems, sems = refs[n * chunks :]
    steps = normed_all.shape[1] // block
    reads = []
    for s in range(steps):
        at = pl.ds(s * block, block)
        copy = pltpu.make_async_copy(normed_all.at[:, at], normed.at[:, at], in_sems.at[s])
        copy.start()
        reads.append(copy)
    arrivals = []
    for c, wide in enumerate(widths):
        for d in range(n):
            ref = terms[d * chunks + c]
            rows = ref.shape[0]
            place = pl.multiple_of(lax.rem(index_ref[0] + d, n) * rows, rows)
            into = turned.at[pl.ds(place, rows), pl.ds(sum(widths[:c]), wide)]
            copy = pltpu.make_async_copy(ref, into, term_sems.at[d * chunks + c])
            copy.start()
            arrivals.append(copy)
    tn = (((0,), (0,)), ((), ()))
    columns = (slice(0, qc), slice(qc, qc + kc), slice(qc + kc, qc + 2 * kc))
    writes = []
    for s in range(steps):
        reads[s].wait()
        x = normed[:, s * block : (s + 1) * block]
        at = pl.ds(s * block, block)
        for i, (buffer, out) in enumerate(zip((bq, bk, bv), (gq, gk, gv))):
            value = lax.dot_general(x, grads[:, columns[i]], tn, preferred_element_type=f32)
            buffer[s * block : (s + 1) * block, :] = value.astype(bf16)
            copy = pltpu.make_async_copy(buffer.at[at], out.at[at], sems.at[s * 3 + i])
            copy.start()
            writes.append(copy)
    for copy in arrivals:
        copy.wait()
    for s in range(steps):
        at = slice(s * block, (s + 1) * block)
        product = normed[:, at].astype(f32) * turned[:, at].astype(f32)
        gg[:, at] = jnp.sum(product, axis=0, keepdims=True) / gain[:, at]
    for copy in writes:
        copy.wait()


def weights(index, grads, gain, normed_all, terms, qc, kc, n, widths):
    length, total = grads.shape
    full = normed_all.shape[1]
    block = step_size(full, WEIGHT_ROWS)
    steps = full // block
    shapes = [(full, qc), (full, kc), (full, kc)]
    return pl.pallas_call(
        functools.partial(weight_kernel, qc, kc, block, n, widths),
        out_shape=[jax.ShapeDtypeStruct(s, bf16) for s in shapes]
        + [jax.ShapeDtypeStruct((1, full), f32)],
        in_specs=[smem(), whole(), whole()] + [anywhere()] * (1 + len(terms)),
        out_specs=[anywhere()] * 3 + [whole()],
        scratch_shapes=[VMEM((length, full), bf16)] * 2
        + [VMEM(s, bf16) for s in shapes]
        + [
            pltpu.SemaphoreType.DMA((steps,)),
            pltpu.SemaphoreType.DMA((len(terms),)),
            pltpu.SemaphoreType.DMA((steps * 3,)),
        ],
        compiler_params=params(26),
        cost_estimate=cost(2 * length * full * total, full * total * 2),
        name="weight_gradients",
    )(index, grads, far(gain), far(normed_all), *[far(t) for t in terms])


def token_kernel(n, widths, x_ref, gain_ref, *refs):
    chunks = len(widths)
    terms, out = refs[:-1], refs[-1]
    x = x_ref[...].astype(f32)
    inverse = lax.rsqrt(jnp.mean(x * x, axis=-1, keepdims=True) + epsilon)
    xhat = x * inverse
    scaled, at = [], 0
    for c, wide in enumerate(widths):
        summed = sum(terms[d * chunks + c][...].astype(f32) for d in range(n))
        scaled.append(summed * gain_ref[:, at : at + wide])
        at += wide
    scaled = jnp.concatenate(scaled, 1)
    mean = jnp.mean(scaled * xhat, axis=-1, keepdims=True)
    out[...] = (inverse * (scaled - xhat * mean)).astype(bf16)


def token_gradient(x, gain, terms, n, widths):
    rows, width = x.shape
    block = rows // TOKEN_STEPS if rows % (16 * TOKEN_STEPS) == 0 else rows
    by_rows = lambda c: pl.BlockSpec((block, c), lambda s: (s, 0))
    fixed = pl.BlockSpec((1, width), lambda s: (0, 0))
    return pl.pallas_call(
        functools.partial(token_kernel, n, widths),
        grid=(rows // block,),
        out_shape=jax.ShapeDtypeStruct(x.shape, bf16),
        in_specs=[by_rows(width), fixed] + [by_rows(w) for w in widths] * n,
        out_specs=by_rows(width),
        compiler_params=params(16),
        cost_estimate=cost(1e9, x.size * 8),
        name="token_gradient",
    )(far(x), far(gain), *terms)


def grid_of(shape, n):
    rows, width = shape
    across = max(1, 8 * n // rows)
    if n % across or rows % (n // across) or width % (across * 128):
        across = 1
    return n // across, across


def cut(array, n):
    down, across = grid_of(array.shape, n)
    rows, width = array.shape
    pieces = array.reshape(down, rows // down, across, width // across)
    return pieces.transpose(0, 2, 1, 3).reshape(n, rows // down, width // across)


def mean_kernel(across, rep_ref, pieces, ours, out, mine_ref, sem):
    n, high, wide = pieces.shape
    row = pl.multiple_of(rep_ref[0] // across * high, high)
    col = pl.multiple_of(lax.rem(rep_ref[0], across) * wide, wide)
    copy = pltpu.make_async_copy(ours.at[pl.ds(row, high), pl.ds(col, wide)], mine_ref, sem)
    copy.start()
    total = jnp.zeros(mine_ref.shape, f32)
    for r in range(n):
        total += pieces[r].astype(f32)
    copy.wait()
    total = (mine_ref[...] - total / n).astype(out.dtype)
    for r in range(n):
        out[r] = total


def mean_pieces(rep, pieces, ours):
    _, across = grid_of(ours.shape, pieces.shape[0])
    return pl.pallas_call(
        functools.partial(mean_kernel, across),
        out_shape=jax.ShapeDtypeStruct(pieces.shape, bf16),
        in_specs=[smem(), whole(), anywhere()],
        out_specs=whole(),
        scratch_shapes=[VMEM(pieces.shape[1:], f32), pltpu.SemaphoreType.DMA],
        compiler_params=params(8),
        cost_estimate=cost(1e8, pieces.size * 6),
        name="mean_pieces",
    )(rep, pieces, far(ours))


def update_kernel(across, pieces, ours, momentum, *rest):
    *gains, new_ours, new_momentum, gain_out = rest
    gain_out[...] = sum(g[...] for g in gains)
    n, high, wide = pieces.shape
    for r in range(n):
        row, col = r // across * high, r % across * wide
        at = slice(row, row + high), slice(col, col + wide)
        mean_delta = pieces[r].astype(f32)
        speed = outer_momentum * momentum[at] + mean_delta
        new_momentum[at] = speed
        new_ours[at] = ours[at] - outer_rate * (mean_delta + outer_momentum * speed)


def update(pieces, ours, momentum, gains):
    _, across = grid_of(ours.shape, pieces.shape[0])
    shapes = [ours.shape, ours.shape, gains[0].shape]
    return pl.pallas_call(
        functools.partial(update_kernel, across),
        out_shape=[jax.ShapeDtypeStruct(s, f32) for s in shapes],
        in_specs=[whole()] * (3 + len(gains)),
        out_specs=[whole()] * 3,
        compiler_params=params(8),
        cost_estimate=cost(1e8, ours.size * 20),
        name="update",
    )(pieces, ours, momentum, *gains)


def send(piece, pairs):
    return lax.ppermute(piece, "tp", pairs)


def step(
    tokens,
    norm_gain,
    w_query,
    key_weight,
    value_weight,
    attention_gradient,
    global_fragment,
    momentum,
    local_fragment,
):
    x, wq, wk, wv = tokens[0], w_query[0], key_weight[0], value_weight[0]
    grad_out = attention_gradient[0]
    n, replicas = lax.axis_size("tp"), lax.axis_size("rep")
    here = lax.axis_index("tp")
    index = here.reshape(1).astype(jnp.int32)
    rows, features = x.shape
    qc, kc = wq.shape[1], wk.shape[1]
    parts, widths = chunk_widths(features, 2), chunk_widths(features, 1)
    chunks = len(widths)
    shift = lambda d: [(j, (j + d) % n) for j in range(n)]

    own = list(norm(x, norm_gain, parts))
    arrived = [[send(piece, shift(d)) for piece in own] for d in range(1, n)]

    tables = rope_tables(rows * n, HEAD_SIZE)
    own_rows, normed_all = project_own(index, own, wq, wk, wv, tables)
    ready = [own_rows]

    rep = lax.axis_index("rep").reshape(1).astype(jnp.int32)
    pieces = lax.all_to_all(cut(local_fragment[0], replicas), "rep", 0, 0, tiled=False)
    spread = mean_pieces(rep, pieces, global_fragment)

    offsets = [sum(parts[:c]) for c in range(chunks)]
    for d in range(1, n):
        acc = None
        owner = lax.rem(index + (n - d), n)
        for c in range(chunks if d < n - 1 else chunks - 1):
            acc, normed_all = project_part(
                owner, arrived[d - 1][c], wq, wk, wv, acc, normed_all, offsets[c]
            )
        if d < n - 1:
            turn = lax.dynamic_slice_in_dim(tables, owner[0] * rows, rows, 0)
            ready.append(finish(acc, turn, qc, kc))
    last = arrived[n - 2][chunks - 1]
    grads, normed_all, *terms = last_and_attention(
        index, last, wq, wk, wv, acc, ready, grad_out, tables, normed_all, offsets[-1], widths[0]
    )

    terms = [terms]
    for c in range(1, chunks):
        terms.append(back(index, grads, wq, wk, wv, n, sum(widths[:c]), widths[c]))
    landed = [[send(terms[c][d], shift(d)) for c in range(chunks)] for d in range(1, n)]
    own_terms = [terms[c][0] for c in range(chunks)]
    ordered = [terms[c][d] for d in range(n) for c in range(chunks)]
    grad_wq, grad_wk, grad_wv, gain_part = weights(
        index, grads, norm_gain, normed_all, ordered, qc, kc, n, widths
    )
    gains = [gain_part] + [send(gain_part, shift(d)) for d in range(1, n)]

    gathered = lax.all_to_all(spread, "rep", 0, 0, tiled=False)
    new_global, new_momentum, gain_total = update(gathered, global_fragment, momentum, gains)

    grad_tokens = token_gradient(
        x, norm_gain, own_terms + [c for group in landed for c in group], n, widths
    )
    return (
        grad_wq[None],
        grad_wk[None],
        grad_wv[None],
        gain_total,
        grad_tokens[None],
        new_global,
        new_momentum,
    )


def finish_kernel(qc, kc, acc, tables, out):
    parts = acc[:, :qc], acc[:, qc : qc + kc], acc[:, qc + kc :]
    finish_projection(parts, tables[...], out, 0)


def finish(acc, tables, qc, kc):
    return pl.pallas_call(
        functools.partial(finish_kernel, qc, kc),
        out_shape=jax.ShapeDtypeStruct(acc.shape, bf16),
        in_specs=[whole()] * 2,
        out_specs=whole(),
        compiler_params=params(8),
        cost_estimate=cost(1e8, acc.size * 6),
        name="finish_projection",
    )(acc, tables)


def solution(mesh):
    placed = (
        P("rep", "tp", None),
        P("rep", None),
        P("rep", None, "tp"),
        P("rep", None, "tp"),
        P("rep", None, "tp"),
        P("rep", None, "tp"),
        P("tp", None),
        P("tp", None),
        P("rep", "tp", None),
    )
    return jax.shard_map(
        step,
        mesh=mesh,
        in_specs=placed,
        out_specs=(
            P("rep", None, "tp"),
            P("rep", None, "tp"),
            P("rep", None, "tp"),
            P("rep", None),
            P("rep", "tp", None),
            P("tp", None),
            P("tp", None),
        ),
        check_vma=False,
    )
```

time: 77.2 us -> 82.6 us (1.070)
  local copies, waits for them, and re-layouts: 9.91 us -> 20.2 us
  Pallas kernels: 36.5 us -> 32.5 us
  waiting for transfers between devices: 10.1 us -> 9.06 us
    unnamed x32 -> x50, local copies, waits for them, and re-layouts: 9.91 us -> 20.2 us
    pallas_call x7 -> x6, Pallas kernels: 24.9 us -> 22.7 us  [the longest x1 7.22 us: weights(): pl.pallas_call(functools.partial(weight_kernel, qc, kc, block, n, widths)...]
    pallas_call x1, Pallas kernels: 8.34 us -> 6.72 us  [project_own(): pl.pallas_call(functools.partial(own_kernel, block, min(3, steps)), out_s...]
    ppermute x5, waiting for transfers between devices: 10.1 us -> 9.05 us  [send(): return lax.ppermute(piece, 'tp', pairs)]
  transfers between devices with their start and end apart: 7 -> 7, of which waited for: 1 -> 1; matrix products, arithmetic and copies ran while one was open for 0% -> 0% of each run, Pallas kernels for 40% -> 33%
where the time goes in v2:
time: 82.6 us; the launch traced here: 81.8 us
  Pallas kernels  32.5 us (39%)
  local copies, waits for them, and re-layouts  20.2 us (24%)
  starting transfers between devices  19.1 us (23%)
  waiting for transfers between devices  9.06 us (11%)
  between operations  0.86 us (1%)
    unnamed x50, local copies, waits for them, and re-layouts  20.2 us
    ppermute x5, waiting for transfers between devices, send(): return lax.ppermute(piece, 'tp', pairs)  9.05 us
    pallas_call x1, Pallas kernels, weights(): pl.pallas_call(functools.partial(weight_kernel, qc, kc, block, n, widths)...  7.22 us
    pallas_call x1, Pallas kernels, project_own(): pl.pallas_call(functools.partial(own_kernel, block, min(3, steps)), out_s...  6.72 us
    ppermute x5, starting transfers between devices, send(): return lax.ppermute(piece, 'tp', pairs)  6.64 us
    all_to_all x1, starting transfers between devices, step(): lax.all_to_all(cut(local_fragment[0], replicas), 'rep', 0, 0, tiled=False)  6.39 us
    all_to_all x1, starting transfers between devices, step(): gathered = lax.all_to_all(spread, 'rep', 0, 0, tiled=False)  6.06 us
    pallas_call x1, Pallas kernels, last_and_attention(): pl.pallas_call(functools.partial(last_kernel, offset, len(ready)), out_sh...  5.05 us
  transfers between devices with their start and end apart: 7, of which 1 were waited for; matrix products, arithmetic and copies ran while one was open for 0% of the time, Pallas kernels for 33%

profile of v2, /device:TPU:0, one launch (start us, length us, event | category | flops | bytes accessed | tf_op | source)
XLA Modules:
  0.0 81.8 jit_solution(2538402802037065952)
XLA Ops:
  0.6 2.4 %norm.1 = (bf16[128,2048]{1,0:T(8,128)(2,1)}, bf16[128,1024]{1,0:T(8,128)(2,1)}) custom-call(bf16[128,3072]{1,0:T(8,128)(2,1)} %bitcast.29, f32[1,3072]{1,0:T(1,128)} %gain_ref.3), custom_call_target="tpu_custom_call" | custom-call | flops 1000000000 | bytes 1572864 | tf_op jit(solution)/shard_map/norm/pallas_call | solution.py:92
  3.0 3.0 %collective-permute-start.1 = (bf16[128,2048]{1,0:T(8,128)(2,1)}, bf16[128,2048]{1,0:T(8,128)(2,1)}, u32[]{:S(2)}, u32[]{:S(2)}) collective-permute-start(bf16[128,2048]{1,0:T(8,128)(2,1)} %get-tuple-element.27.refs_0_), channel_id=1, source_target_pairs={{0,1},{1,0},{2,3},{3,2},{4,5},{5,4},{6,7},{7,6},{8,9},{9,8},{10,11... | collective-permute-start | bytes 1572872 | tf_op jit(solution)/shard_map/ppermute | solution.py:565
  6.0 0.0 collective-permute-start
  6.1 6.4 %all-to-all-start = ((bf16[16,8,1536]{2,1,0:T(8,128)(2,1)}), bf16[16,8,1536]{2,1,0:T(8,128)(2,1)S(1)}, u32[]{:S(2)}, u32[]{:S(2)}) async-start(bf16[16,8,1536]{2,1,0:T(8,128)(2,1)} %bitcast.12), calls=%async_computation | async-start | bytes 786432 | tf_op jit(solution)/shard_map/all_to_all | solution.py:598
  12.5 0.0 copy-start.16
  12.5 0.9 %copy-done.16 = f32[256,256]{1,0:T(8,128)S(1)} copy-done((f32[256,256]{1,0:T(8,128)S(1)}, f32[256,256]{1,0:T(8,128)}, u32[]{:S(2)}) %copy-start.16) | copy-done | bytes 262168
  13.4 6.7 %own_projection.1 = (bf16[128,2048]{1,0:T(8,128)(2,1)S(1)}, bf16[256,3072]{1,0:T(8,128)(2,1)S(1)}) custom-call(s32[1]{0:T(128)} %bitcast.index_ref, f32[256,256]{1,0:T(8,128)S(1)} %copy-done.16, bf16[128,2048]{1,0:T(8,128)(2,1)} %get-tuple-element.27.refs_0_, bf16[128,1024]{1,0:T(8,128)(2,1)} %get-tuple-element.26.refs_1_, bf16[3072,1024]{1,0:T(8,128)(2,1)} %bitcast.16, ...), custom_call_target="tpu_custom_call" | custom-call | flops 5000000000 | bytes 12582912 | tf_op jit(solution)/shard_map/own_projection/pallas_call | solution.py:184
  20.2 1.2 %copy-done.7 = bf16[256,3072]{1,0:T(8,128)(2,1)} copy-done((bf16[256,3072]{1,0:T(8,128)(2,1)}, bf16[256,3072]{1,0:T(8,128)(2,1)S(1)}, u32[]{:S(2)}) %copy-start.7) | copy-done | bytes 1572888
  21.3 0.8 copy-done.14
  22.1 0.0 collective-permute-done.1.chunk
  22.1 2.8 %copy-done = bf16[1,3072,1024]{2,1,0:T(8,128)(2,1)S(1)} copy-done((bf16[1,3072,1024]{2,1,0:T(8,128)(2,1)S(1)}, bf16[1,3072,1024]{2,1,0:T(8,128)(2,1)}, u32[]{:S(2)}) %copy-start) | copy-done | bytes 6291480
  24.9 1.9 %copy-done.4 = bf16[1,3072,512]{2,1,0:T(8,128)(2,1)S(1)} copy-done((bf16[1,3072,512]{2,1,0:T(8,128)(2,1)S(1)}, bf16[1,3072,512]{2,1,0:T(8,128)(2,1)}, u32[]{:S(2)}) %copy-start.4) | copy-done | bytes 3145752
  26.8 2.9 %part_projection.1 = (f32[128,2048]{1,0:T(8,128)S(1)}, bf16[256,3072]{1,0:T(8,128)(2,1)}) custom-call(s32[1]{0:T(128)S(6)} %rem.18.row_ref, bf16[128,2048]{1,0:T(8,128)(2,1)} %collective-permute-done.1.chunk, bf16[3072,1024]{1,0:T(8,128)(2,1)S(1)} %bitcast.17, bf16[3072,512]{1,0:T(8,128)(2,1)S(1)} %bitcast.21, ...), custom_call_target="tpu_custom_call", output_to_operand_aliasing={{1}: (5, {})} | custom-call | flops 1073741824 | bytes 8388608 | tf_op jit(solution)/shard_map/part_projection/pallas_call | solution.py:224
  29.7 0.0 collective-permute-done.chunk
  29.7 0.0 copy-done.5
  29.7 0.0 copy-done.13
  29.7 0.0 copy-done.15
  29.7 0.0 copy-start.1
  29.8 2.8 %copy-done.1 = bf16[1,3072,1024]{2,1,0:T(8,128)(2,1)S(1)} copy-done((bf16[1,3072,1024]{2,1,0:T(8,128)(2,1)S(1)}, bf16[1,3072,1024]{2,1,0:T(8,128)(2,1)}, u32[]{:S(2)}) %copy-start.1) | copy-done | bytes 6291480
  32.5 5.1 %attention.1 = (bf16[256,2048]{1,0:T(8,128)(2,1)S(1)}, bf16[256,3072]{1,0:T(8,128)(2,1)}, bf16[128,1024]{1,0:T(8,128)(2,1)S(1)}, bf16[128,1024]{1,0:T(8,128)(2,1)S(1)}) custom-call(s32[1]{0:T(128)} %bitcast.index_ref, bf16[128,1024]{1,0:T(8,128)(2,1)} %collective-permute-done.chunk, ...), custom_call_target="tpu_custom_call", output_to_operand_aliasing={{1}: (9, {})} | custom-call | flops 4000000000 | bytes 4194304 | tf_op jit(solution)/shard_map/attention/pallas_call | solution.py:335
  37.6 0.0 copy-start.10
  37.6 1.0 %copy-done.10 = bf16[256,2048]{1,0:T(8,128)(2,1)} copy-done((bf16[256,2048]{1,0:T(8,128)(2,1)}, bf16[256,2048]{1,0:T(8,128)(2,1)S(1)}, u32[]{:S(2)}) %copy-start.10) | copy-done | bytes 1048600
  38.6 0.7 copy-done.21
  39.3 0.7 copy-done.23
  40.0 0.0 all-to-all-done.pieces
  40.0 0.8 %mean_pieces.1 = bf16[16,8,1536]{2,1,0:T(8,128)(2,1)S(1)} custom-call(s32[1]{0:T(128)} %bitcast.9.rep_ref, bf16[16,8,1536]{2,1,0:T(8,128)(2,1)S(1)} %all-to-all-done.pieces, f32[64,3072]{1,0:T(8,128)} %ours.3), custom_call_target="tpu_custom_call" | custom-call | flops 100000000 | bytes 1179648 | tf_op jit(solution)/shard_map/mean_pieces/pallas_call | solution.py:525
  40.9 0.0 copy-start.9
  40.9 0.7 copy-done.9
  41.6 6.1 %all-to-all-start.1 = ((bf16[16,8,1536]{2,1,0:T(8,128)(2,1)}), bf16[16,8,1536]{2,1,0:T(8,128)(2,1)}, u32[]{:S(2)}, u32[]{:S(2)}) async-start(bf16[16,8,1536]{2,1,0:T(8,128)(2,1)} %copy-done.9), calls=%async_computation.1 | async-start | bytes 786432 | tf_op jit(solution)/shard_map/all_to_all | solution.py:628
  47.7 0.0 copy-start.2
  47.7 2.8 %copy-done.2 = bf16[1,3072,1024]{2,1,0:T(8,128)(2,1)S(1)} copy-done((bf16[1,3072,1024]{2,1,0:T(8,128)(2,1)S(1)}, bf16[1,3072,1024]{2,1,0:T(8,128)(2,1)}, u32[]{:S(2)}) %copy-start.2) | copy-done | bytes 6291480
  50.5 1.9 %copy-done.6 = bf16[1,3072,512]{2,1,0:T(8,128)(2,1)S(1)} copy-done((bf16[1,3072,512]{2,1,0:T(8,128)(2,1)S(1)}, bf16[1,3072,512]{2,1,0:T(8,128)(2,1)}, u32[]{:S(2)}) %copy-start.6) | copy-done | bytes 3145752
  52.4 1.2 %copy-done.11 = bf16[256,2048]{1,0:T(8,128)(2,1)S(1)} copy-done((bf16[256,2048]{1,0:T(8,128)(2,1)S(1)}, bf16[256,2048]{1,0:T(8,128)(2,1)}, u32[]{:S(2)}) %copy-start.11) | copy-done | bytes 1048600
  53.6 2.5 %back_projection.1 = (bf16[128,2048]{1,0:T(8,128)(2,1)S(1)}, bf16[128,2048]{1,0:T(8,128)(2,1)S(1)}) custom-call(s32[1]{0:T(128)} %bitcast.index_ref, bf16[256,2048]{1,0:T(8,128)(2,1)S(1)} %copy-done.11, bf16[3072,1024]{1,0:T(8,128)(2,1)S(1)} %bitcast.19, bf16[3072,512]{1,0:T(8,128)(2,1)S(1)} %bitcast.23, bf16[3072,512]{1,0:T(8,128)(2,1)S(1)} %bitcast.27), custom_call_target="tpu_custom_call" | custom-call | flops 2147483648 | bytes 8388608 | tf_op jit(solution)/shard_map/back_projection/pallas_call | solution.py:379
  56.1 0.0 copy-start.18
  56.1 0.8 copy-done.18
  56.9 1.5 %collective-permute-start.4 = (bf16[128,2048]{1,0:T(8,128)(2,1)S(1)}, bf16[128,2048]{1,0:T(8,128)(2,1)S(1)}, u32[]{:S(2)}, u32[]{:S(2)}) collective-permute-start(bf16[128,2048]{1,0:T(8,128)(2,1)S(1)} %get-tuple-element.37.refs_3_), channel_id=1, source_target_pairs={{0,1},{1,0},{2,3},{3,2},{4,5},{5,4},{6,7},{7,6},{8,9},{9,8},{10,11... | collective-permute-start | bytes 1572872 | tf_op jit(solution)/shard_map/ppermute | solution.py:565
  58.4 0.5 collective-permute-start.3
  58.9 7.2 %weight_gradients.1 = (bf16[3072,1024]{1,0:T(8,128)(2,1)}, bf16[3072,512]{1,0:T(8,128)(2,1)}, bf16[3072,512]{1,0:T(8,128)(2,1)}, f32[1,3072]{1,0:T(1,128)S(1)}) custom-call(s32[1]{0:T(128)} %bitcast.index_ref, bf16[256,2048]{1,0:T(8,128)(2,1)S(1)} %copy-done.11, f32[1,3072]{1,0:T(1,128)} %gain_ref.3, bf16[256,3072]{1,0:T(8,128)(2,1)} %get-tuple-element.33.normed_all, ...), custom_call_target="tpu_custom_call" | custom-call | flops 3221225472 | bytes 12582912 | tf_op jit(solution)/shard_map/weight_gradients/pallas_call | solution.py:441
  66.1 0.0 copy-start.8
  66.1 0.0 copy-start.12
  66.1 1.6 %collective-permute-start.2 = (f32[1,3072]{1,0:T(1,128)S(1)}, f32[1,3072]{1,0:T(1,128)S(1)}, u32[]{:S(2)}, u32[]{:S(2)}) collective-permute-start(f32[1,3072]{1,0:T(1,128)S(1)} %get-tuple-element.41.rest_0_), channel_id=1, source_target_pairs={{0,1},{1,0},{2,3},{3,2},{4,5},{5,4},{6,7},{7,6},{8,9},{9,8},{10,11... | collective-permute-start | bytes 36872 | tf_op jit(solution)/shard_map/ppermute | solution.py:565
  67.7 9.0 %collective-permute-done.3.refs_2_ = bf16[128,1024]{1,0:T(8,128)(2,1)S(1)} collective-permute-done((bf16[128,1024]{1,0:T(8,128)(2,1)S(1)}, bf16[128,1024]{1,0:T(8,128)(2,1)S(1)}, u32[]{:S(2)}, u32[]{:S(2)}) %collective-permute-start.3) | collective-permute-done | bytes 262176 | tf_op jit(solution)/shard_map/ppermute | solution.py:565
  76.8 0.0 collective-permute-done.4.refs_3_
  76.8 2.7 %token_gradient.1 = bf16[128,3072]{1,0:T(8,128)(2,1)} custom-call(bf16[128,3072]{1,0:T(8,128)(2,1)} %bitcast.30, f32[1,3072]{1,0:T(1,128)} %gain_ref.3, bf16[128,1024]{1,0:T(8,128)(2,1)S(1)} %copy-done.22, bf16[128,2048]{1,0:T(8,128)(2,1)S(1)} %copy-done.19, bf16[128,1024]{1,0:T(8,128)(2,1)S(1)} %collective-permute-done.3.refs_2_, ...), custom_call_target="tpu_custom_call" | custom-call | flops 1000000000 | bytes 3145728 | tf_op jit(solution)/shard_map/token_gradient/pallas_call | solution.py:481
  79.5 0.0 collective-permute-done.2.rest_1_
  79.5 0.0 all-to-all-done.1.pieces
  79.5 2.3 %update.1 = (f32[64,3072]{1,0:T(8,128)}, f32[64,3072]{1,0:T(8,128)}, f32[1,3072]{1,0:T(1,128)}) custom-call(bf16[16,8,1536]{2,1,0:T(8,128)(2,1)} %all-to-all-done.1.pieces, f32[64,3072]{1,0:T(8,128)S(1)} %copy-done.8, f32[64,3072]{1,0:T(8,128)S(1)} %copy-done.12, f32[1,3072]{1,0:T(1,128)S(1)} %get-tuple-element.41.rest_0_, ...), custom_call_target="tpu_custom_call" | custom-call | flops 100000000 | bytes 3932160 | tf_op jit(solution)/shard_map/update/pallas_call | solution.py:553
  (25 shorter events, 0.0 us)
Async XLA Ops:
  3.0 19.1 %collective-permute-start.1 = (bf16[128,2048]{1,0:T(8,128)(2,1)}, bf16[128,2048]{1,0:T(8,128)(2,1)}, u32[]{:S(2)}, u32[]{:S(2)}) collective-permute-start(bf16[128,2048]{1,0:T(8,128)(2,1)} %get-tuple-element.27.refs_0_), channel_id=1, source_target_pairs={{0,1},{1,0},{2,3},{3,2},{4,5},{5,4},{6,7},{7,6},{8,9},{9,8},{10,11... | collective-permute-start | bytes 1572872 | tf_op jit(solution)/shard_map/ppermute | solution.py:565
  6.0 23.7 %collective-permute-start = (bf16[128,1024]{1,0:T(8,128)(2,1)}, bf16[128,1024]{1,0:T(8,128)(2,1)}, u32[]{:S(2)}, u32[]{:S(2)}) collective-permute-start(bf16[128,1024]{1,0:T(8,128)(2,1)} %get-tuple-element.26.refs_1_), channel_id=1, source_target_pairs={{0,1},{1,0},{2,3},{3,2},{4,5},{5,4},{6,7},{7,6},{8,9},{9,8},{10,11... | collective-permute-start | bytes 786440 | tf_op jit(solution)/shard_map/ppermute | solution.py:565
  6.1 34.0 %all-to-all-start = ((bf16[16,8,1536]{2,1,0:T(8,128)(2,1)}), bf16[16,8,1536]{2,1,0:T(8,128)(2,1)S(1)}, u32[]{:S(2)}, u32[]{:S(2)}) async-start(bf16[16,8,1536]{2,1,0:T(8,128)(2,1)} %bitcast.12), calls=%async_computation | async-start | bytes 786432 | tf_op jit(solution)/shard_map/all_to_all | solution.py:598
  12.5 1.0 %copy-start.16 = (f32[256,256]{1,0:T(8,128)S(1)}, f32[256,256]{1,0:T(8,128)}, u32[]{:S(2)}) copy-start(f32[256,256]{1,0:T(8,128)} %constant.18.clone.tables.rest_3_) | copy-start | bytes 786436
  13.4 8.7 %copy-start.3 = (bf16[1,3072,512]{2,1,0:T(8,128)(2,1)S(1)}, bf16[1,3072,512]{2,1,0:T(8,128)(2,1)}, u32[]{:S(2)}) copy-start(bf16[1,3072,512]{2,1,0:T(8,128)(2,1)} %param.13) | copy-start | bytes 9437188
  20.1 1.2 %copy-start.7 = (bf16[256,3072]{1,0:T(8,128)(2,1)}, bf16[256,3072]{1,0:T(8,128)(2,1)S(1)}, u32[]{:S(2)}) copy-start(bf16[256,3072]{1,0:T(8,128)(2,1)S(1)} %get-tuple-element.28.rest_0_) | copy-start | bytes 4718596
  21.3 0.8 copy-start.14
  22.1 2.8 %copy-start = (bf16[1,3072,1024]{2,1,0:T(8,128)(2,1)S(1)}, bf16[1,3072,1024]{2,1,0:T(8,128)(2,1)}, u32[]{:S(2)}) copy-start(bf16[1,3072,1024]{2,1,0:T(8,128)(2,1)} %param.12) | copy-start | bytes 18874372
  24.9 1.9 %copy-start.4 = (bf16[1,3072,512]{2,1,0:T(8,128)(2,1)S(1)}, bf16[1,3072,512]{2,1,0:T(8,128)(2,1)}, u32[]{:S(2)}) copy-start(bf16[1,3072,512]{2,1,0:T(8,128)(2,1)} %param.14) | copy-start | bytes 9437188
  26.8 2.9 %copy-start.5 = (bf16[1,3072,512]{2,1,0:T(8,128)(2,1)S(1)}, bf16[1,3072,512]{2,1,0:T(8,128)(2,1)}, u32[]{:S(2)}) copy-start(bf16[1,3072,512]{2,1,0:T(8,128)(2,1)} %param.14) | copy-start | bytes 9437188
  26.8 2.9 %copy-start.13 = (bf16[1,256,1024]{2,1,0:T(8,128)(2,1)S(1)}, bf16[1,256,1024]{2,1,0:T(8,128)(2,1)}, u32[]{:S(2)}) copy-start(bf16[1,256,1024]{2,1,0:T(8,128)(2,1)} %param.15) | copy-start | bytes 1572868
  26.8 2.9 %copy-start.15 = (bf16[128,2048]{1,0:T(8,128)(2,1)S(1)}, bf16[128,2048]{1,0:T(8,128)(2,1)}, u32[]{:S(2)}) copy-start(bf16[128,2048]{1,0:T(8,128)(2,1)} %copy-done.14) | copy-start | bytes 1572868
  26.8 2.9 %copy-start.17 = (f32[256,256]{1,0:T(8,128)S(1)}, f32[256,256]{1,0:T(8,128)}, u32[]{:S(2)}) copy-start(f32[256,256]{1,0:T(8,128)} %constant.18.clone.tables.rest_3_) | copy-start | bytes 786436
  29.7 2.8 %copy-start.1 = (bf16[1,3072,1024]{2,1,0:T(8,128)(2,1)S(1)}, bf16[1,3072,1024]{2,1,0:T(8,128)(2,1)}, u32[]{:S(2)}) copy-start(bf16[1,3072,1024]{2,1,0:T(8,128)(2,1)} %param.12) | copy-start | bytes 18874372
  37.6 1.0 %copy-start.10 = (bf16[256,2048]{1,0:T(8,128)(2,1)}, bf16[256,2048]{1,0:T(8,128)(2,1)S(1)}, u32[]{:S(2)}) copy-start(bf16[256,2048]{1,0:T(8,128)(2,1)S(1)} %get-tuple-element.32.grads) | copy-start | bytes 3145732
  38.6 0.7 copy-start.21
  39.3 0.7 copy-start.23
  40.9 0.7 copy-start.9
  41.6 37.9 %all-to-all-start.1 = ((bf16[16,8,1536]{2,1,0:T(8,128)(2,1)}), bf16[16,8,1536]{2,1,0:T(8,128)(2,1)}, u32[]{:S(2)}, u32[]{:S(2)}) async-start(bf16[16,8,1536]{2,1,0:T(8,128)(2,1)} %copy-done.9), calls=%async_computation.1 | async-start | bytes 786432 | tf_op jit(solution)/shard_map/all_to_all | solution.py:628
  47.7 2.8 %copy-start.2 = (bf16[1,3072,1024]{2,1,0:T(8,128)(2,1)S(1)}, bf16[1,3072,1024]{2,1,0:T(8,128)(2,1)}, u32[]{:S(2)}) copy-start(bf16[1,3072,1024]{2,1,0:T(8,128)(2,1)} %param.12) | copy-start | bytes 18874372
  50.5 1.9 %copy-start.6 = (bf16[1,3072,512]{2,1,0:T(8,128)(2,1)S(1)}, bf16[1,3072,512]{2,1,0:T(8,128)(2,1)}, u32[]{:S(2)}) copy-start(bf16[1,3072,512]{2,1,0:T(8,128)(2,1)} %param.14) | copy-start | bytes 9437188
  52.4 1.2 %copy-start.11 = (bf16[256,2048]{1,0:T(8,128)(2,1)S(1)}, bf16[256,2048]{1,0:T(8,128)(2,1)}, u32[]{:S(2)}) copy-start(bf16[256,2048]{1,0:T(8,128)(2,1)} %copy-done.10) | copy-start | bytes 3145732
  53.6 4.8 %copy-start.24 = (bf16[128,1024]{1,0:T(8,128)(2,1)S(1)}, bf16[128,1024]{1,0:T(8,128)(2,1)}, u32[]{:S(2)}) copy-start(bf16[128,1024]{1,0:T(8,128)(2,1)} %copy-done.23) | copy-start | bytes 786436
  56.1 0.8 copy-start.18
  56.9 2.0 %copy-start.20 = (bf16[128,2048]{1,0:T(8,128)(2,1)}, bf16[128,2048]{1,0:T(8,128)(2,1)S(1)}, u32[]{:S(2)}) copy-start(bf16[128,2048]{1,0:T(8,128)(2,1)S(1)} %get-tuple-element.37.refs_3_) | copy-start | bytes 1572868
  56.9 19.9 %collective-permute-start.4 = (bf16[128,2048]{1,0:T(8,128)(2,1)S(1)}, bf16[128,2048]{1,0:T(8,128)(2,1)S(1)}, u32[]{:S(2)}, u32[]{:S(2)}) collective-permute-start(bf16[128,2048]{1,0:T(8,128)(2,1)S(1)} %get-tuple-element.37.refs_3_), channel_id=1, source_target_pairs={{0,1},{1,0},{2,3},{3,2},{4,5},{5,4},{6,7},{7,6},{8,9},{9,8},{10,11... | collective-permute-start | bytes 1572872 | tf_op jit(solution)/shard_map/ppermute | solution.py:565
  58.4 18.4 %collective-permute-start.3 = (bf16[128,1024]{1,0:T(8,128)(2,1)S(1)}, bf16[128,1024]{1,0:T(8,128)(2,1)S(1)}, u32[]{:S(2)}, u32[]{:S(2)}) collective-permute-start(bf16[128,1024]{1,0:T(8,128)(2,1)S(1)} %copy-done.24), channel_id=1, source_target_pairs={{0,1},{1,0},{2,3},{3,2},{4,5},{5,4},{6,7},{7,6},{8,9},{9,8},{10,11... | collective-permute-start | bytes 786440 | tf_op jit(solution)/shard_map/ppermute | solution.py:565
  58.9 17.9 %copy-start.19 = (bf16[128,2048]{1,0:T(8,128)(2,1)S(1)}, bf16[128,2048]{1,0:T(8,128)(2,1)}, u32[]{:S(2)}) copy-start(bf16[128,2048]{1,0:T(8,128)(2,1)} %copy-done.18) | copy-start | bytes 1572868
  58.9 17.9 %copy-start.22 = (bf16[128,1024]{1,0:T(8,128)(2,1)S(1)}, bf16[128,1024]{1,0:T(8,128)(2,1)}, u32[]{:S(2)}) copy-start(bf16[128,1024]{1,0:T(8,128)(2,1)} %copy-done.21) | copy-start | bytes 786436
  66.1 13.4 %copy-start.8 = (f32[64,3072]{1,0:T(8,128)S(1)}, f32[64,3072]{1,0:T(8,128)}, u32[]{:S(2)}) copy-start(f32[64,3072]{1,0:T(8,128)} %ours.3) | copy-start | bytes 2359300
  66.1 13.4 %copy-start.12 = (f32[64,3072]{1,0:T(8,128)S(1)}, f32[64,3072]{1,0:T(8,128)}, u32[]{:S(2)}) copy-start(f32[64,3072]{1,0:T(8,128)} %momentum.1) | copy-start | bytes 2359300
  66.1 13.4 %collective-permute-start.2 = (f32[1,3072]{1,0:T(1,128)S(1)}, f32[1,3072]{1,0:T(1,128)S(1)}, u32[]{:S(2)}, u32[]{:S(2)}) collective-permute-start(f32[1,3072]{1,0:T(1,128)S(1)} %get-tuple-element.41.rest_0_), channel_id=1, source_target_pairs={{0,1},{1,0},{2,3},{3,2},{4,5},{5,4},{6,7},{7,6},{8,9},{9,8},{10,11... | collective-permute-start | bytes 36872 | tf_op jit(solution)/shard_map/ppermute | solution.py:565
